TPU v7x, 128 devices: a whole 4x4x4 slice. The times are simulated.
128 devices in a mesh: mp: 2 (over core), tile: 64 (over x, y, z).
Axes of the slice: x: 4, y: 4, z: 4, core: 2. Of those that a mesh axis runs over, the one named last changes fastest.
Arguments:
- state: float32 [2, 20, 256, 4096], P('mp', None, 'tile'), may hold values from -6 to 6
- guess: float32 [2, 24, 256, 4096], P('mp', None, 'tile'), may hold values from -6 to 6
- regrid: bfloat16 [2, 64, 64, 256, 256], P('mp', 'tile'), may hold values from -1 to 1
- regime: int32 [2, 256, 4096], P('mp', 'tile'), may hold values from 0 to 3
- land: int32 [2, 256, 4096], P('mp', 'tile'), may hold values 0 or 1
- land_temp: float32 [2, 256, 4096], P('mp', 'tile'), may hold values from -6 to 6
- exchange_rate: float32 [2, 4], P('mp'), may hold values from 0.05 to 0.3
- vertical: float32 [2, 19], P('mp'), may hold values from 0.05 to 0.3
- mixing: float32 [2], P('mp'), may hold values from 0.02 to 0.1
Outputs:
- final_state: float32 [2, 20, 256, 4096], P('mp', None, 'tile')
- forcing: float32 [2, 24, 256, 4096], P('mp', None, 'tile')
All inputs are finite; a program needn't handle non-finite values. No bound on the sum of `land` on one device may be relied on, other than what follows from the above.
Results may differ from a plain program's by a relative error of at most 0.0029.
Values may be sent and summed in bfloat16 or wider, within the bound.
A program may use at most 128 MiB of HBM per device.

v0:
```python
import jax
import jax.numpy as jnp
from jax import lax
from jax.sharding import PartitionSpec as P

ITERS = 2


def padded_2(array, sides, width):
    for axis, dim in sides:
        count, length = (lax.axis_size(axis), array.shape[dim])
        up = [(i, (i + 1) % count) for i in range(count - 1)]
        down = [(j, i) for i, j in up]
        last = lax.slice_in_dim(array, length - width, length, axis=dim)
        initial = lax.slice_in_dim(array, 0, width, axis=dim)
        before = lax.ppermute(last, axis, up)
        after = lax.ppermute(initial, axis, down)
        array = jnp.concatenate([before, array, after], axis=dim)
    return array


def from_partner(block, axis, bit):
    count = lax.axis_size(axis)
    route = []
    for low in range(count):
        high = low | 1 << bit
        if high != low and high < count:
            route += [(low, high), (high, low)]
    return lax.ppermute(block, axis, route)


def rate_field(regime, rates):
    field = jnp.zeros(regime.shape, jnp.float32)
    for kind_index in range(rates.shape[0]):
        field = field + jnp.where(
            regime == kind_index, rates[kind_index], jnp.zeros((), jnp.float32)
        )
    return field


def on_device(state, guess, regrid, regime, land, land_temp, exchange_rate, vertical, mixing):
    rows = state.shape[2]
    width = state.shape[3]
    steps = guess.shape[1]
    tiles = lax.axis_size("tile")
    face = width // tiles
    coeff = rate_field(regime[0], exchange_rate[0])
    land_local = land[0]
    land_value = land_temp[0]
    level_mix = vertical[0]
    surface_mix = mixing[0]
    blocks = regrid[0, 0].reshape(tiles, rows, face, rows, face)

    def one_step(carry, force_now):
        surface = carry[0]
        boundary = jnp.where(land_local == 1, land_value, force_now)
        flux = coeff * (boundary - surface)
        padded = padded_2(surface, (("tile", 0),), 1)
        lateral = (
            padded[2:]
            + padded[:-2]
            + jnp.roll(surface, 1, axis=1)
            + jnp.roll(surface, -1, axis=1)
            - 4.0 * surface
        )
        between = level_mix[:, None, None] * (carry[1:] - carry[:-1])
        change = jnp.pad(between, ((0, 1), (0, 0), (0, 0))) - jnp.pad(
            between, ((1, 0), (0, 0), (0, 0))
        )
        updated = carry + change
        updated = updated.at[0].add(flux + surface_mix * lateral)
        return (updated, updated[0].astype(jnp.bfloat16))

    forcing = guess[0]
    column = state[0]
    for sweep_index in range(ITERS):
        column, trace = lax.scan(one_step, state[0], forcing)
        shaped = trace.reshape(steps, rows, tiles, face)
        partner = from_partner(shaped, "mp", 0)
        arrived = lax.all_to_all(partner, "tile", split_axis=2, concat_axis=2, tiled=True)
        mapped = jnp.einsum("traw,apqrw->tpaq", arrived, blocks, preferred_element_type=jnp.float32)
        forcing = mapped.reshape(steps, rows, width)
    return (column[None], forcing[None])


def solution(mesh):
    return jax.shard_map(
        on_device,
        mesh=mesh,
        in_specs=(
            P("mp", None, "tile", None),
            P("mp", None, "tile", None),
            P("mp", "tile", None, None, None),
            P("mp", "tile", None),
            P("mp", "tile", None),
            P("mp", "tile", None),
            P("mp", None),
            P("mp", None),
            P("mp"),
        ),
        out_specs=(P("mp", None, "tile", None), P("mp", None, "tile", None)),
        check_vma=False,
    )
```

profile of v0, /device:TPU:1, one launch (start us, length us, event | category | flops | bytes accessed | tf_op | source)
XLA Modules:
  0.0 807.0 jit_solution(4814524432590251101)
XLA Ops:
  7.3 285.2 %while.30 = (s32[]{:T(128)}, f32[20,4,4096]{2,1,0:T(4,128)S(1)}, bf16[24,4,4096]{2,1,0:T(4,128)(2,1)}, f32[1,19]{1,0:T(1,128)S(1)}, s32[4,4096]{1,0:T(4,128)S(1)...) while((s32[]{:T(128)}, f32[20,4,4096]{2,1,0:T(4,128)S(1)}, ...), condition=%wide.region_1.2_spmd, body=%wide.region_0.1_spmd.sunk | while | flops 1556482 | bytes 8979213 | solution.py:77
  7.4 4.4 collective-permute-start
  18.7 3.4 collective-permute-start
  28.9 3.9 collective-permute-start
  39.6 4.0 collective-permute-start
  50.6 3.9 collective-permute-start
  61.2 4.0 collective-permute-start
  72.1 4.0 collective-permute-start
  82.9 4.0 collective-permute-start
  93.7 4.0 collective-permute-start
  104.5 4.0 collective-permute-start
  115.8 3.6 collective-permute-start
  126.6 3.9 collective-permute-start
  137.5 6.0 collective-permute-start
  150.7 5.7 collective-permute-start
  163.6 5.7 collective-permute-start
  176.6 5.7 collective-permute-start
  189.5 5.7 collective-permute-start
  202.4 5.7 collective-permute-start
  215.7 5.5 collective-permute-start
  228.3 5.7 collective-permute-start
  241.1 5.8 collective-permute-start
  253.8 6.1 collective-permute-start
  267.0 5.8 collective-permute-start
  279.6 6.1 collective-permute-start
  292.5 3.4 reshape.145
  298.3 28.6 %collective-permute-start.4 = (bf16[24,4,64,64]{3,0,1,2:T(8,128)(2,1)S(1)}, bf16[24,4,64,64]{3,0,1,2:T(8,128)(2,1)S(1)}, u32[]{:S(2)}, u32[]{:S(2)}) collective-permute-start(bf16[24,4,64,64]{3,0,1,2:T(8,128)(2,1)S(1)} %copy.14), channel_id=1, source_target_pairs={{0,64},{64,0},{1,65},{65,1},{2,66},{66,2},{3,67},{67,3},{4,68},{68... | collective-permute-start | bytes 2359304 | tf_op jit(solution)/shard_map/ppermute | solution.py:29
  327.0 3.0 collective-permute-done.4
  331.1 3.8 reshape.149
  334.9 36.9 %all-to-all-start = ((bf16[64,2,3072]{2,1,0:T(2,128)(2,1)}), bf16[64,2,3072]{2,1,0:T(2,128)(2,1)S(1)}, u32[]{:S(2)}, u32[]{:S(2)}) async-start(bf16[64,2,3072]{2,1,0:T(2,128)(2,1)} %reshape.149), calls=%async_computation | async-start | bytes 1572864 | tf_op jit(solution)/shard_map/all_to_all | solution.py:80
  371.8 24.5 %reshape_squeeze.3 = bf16[64,4,64,4,64]{4,3,2,1,0:T(4,128)(2,1)} reshape(bf16[1,1,64,256,256]{4,3,2,1,0:T(8,128)(2,1)} %param.19) | data formatting | bytes 16777216 | tf_op jit(solution)/shard_map/reshape;squeeze | solution.py:52
  398.2 14.5 %fusion.24 = f32[24,4,64,64]{3,0,1,2:T(8,128)} fusion(bf16[64,4,64,4,64]{4,3,2,1,0:T(4,128)(2,1)} %reshape_squeeze.3, bf16[64,4,24,64]{3,2,1,0:T(8,128)(2,1)} %reshape.150), kind=kOutput, calls=%fused_computation.44 | convolution fusion | flops 201326592 | bytes 10747904 | tf_op jit(solution)/shard_map/traw,apqrw->tpaq/dot_general | solution.py:81
  412.7 5.4 copy.29
  418.0 3.9 reshape.146
  422.3 269.6 %while.31 = (s32[]{:T(128)}, f32[20,4,4096]{2,1,0:T(4,128)S(1)}, bf16[24,4,4096]{2,1,0:T(4,128)(2,1)S(1)}, f32[1,19]{1,0:T(1,128)S(1)}, s32[4,4096]{1,0:T(4,128)...) while((s32[]{:T(128)}, f32[20,4,4096]{2,1,0:T(4,128)S(1)}, ...), condition=%wide.region_3.4_spmd, body=%wide.region_2.3_spmd.sunk | while | flops 1556482 | bytes 8982801 | solution.py:77
  431.3 3.1 collective-permute-start.2
  440.6 4.6 collective-permute-start.2
  451.4 4.3 collective-permute-start.2
  461.9 3.8 collective-permute-start.2
  471.9 4.0 collective-permute-start.2
  482.1 4.0 collective-permute-start.2
  492.3 4.0 collective-permute-start.2
  502.6 4.0 collective-permute-start.2
  512.9 4.0 collective-permute-start.2
  523.1 4.0 collective-permute-start.2
  533.2 4.3 collective-permute-start.2
  543.8 5.8 collective-permute-start.2
  556.2 5.7 collective-permute-start.2
  568.5 5.7 collective-permute-start.2
  580.9 5.7 collective-permute-start.2
  593.2 5.7 collective-permute-start.2
  605.9 5.5 collective-permute-start.2
  617.9 5.7 collective-permute-start.2
  630.1 5.8 collective-permute-start.2
  642.2 6.1 collective-permute-start.2
  654.8 5.8 collective-permute-start.2
  666.9 6.1 collective-permute-start.2
  679.2 6.6 collective-permute-start.2
  696.8 29.1 %collective-permute-start.5 = (bf16[24,4,64,64]{3,0,1,2:T(8,128)(2,1)S(1)}, bf16[24,4,64,64]{3,0,1,2:T(8,128)(2,1)S(1)}, u32[]{:S(2)}, u32[]{:S(2)}) collective-permute-start(bf16[24,4,64,64]{3,0,1,2:T(8,128)(2,1)S(1)} %copy.19), channel_id=1, source_target_pairs={{0,64},{64,0},{1,65},{65,1},{2,66},{66,2},{3,67},{67,3},{4,68},{68... | collective-permute-start | bytes 2359304 | tf_op jit(solution)/shard_map/ppermute | solution.py:29
  725.9 3.0 collective-permute-done.5
  729.8 51.1 %all_to_all.10 = bf16[64,2,3072]{2,1,0:T(2,128)(2,1)} all-to-all(bf16[64,2,3072]{2,1,0:T(2,128)(2,1)S(1)} %reshape.151), channel_id=1, replica_groups=mesh['mp'=2,'tile'=64] {'tile'}, dimensions={0} | all-to-all | bytes 1572864 | tf_op jit(solution)/shard_map/all_to_all | solution.py:80
  783.8 14.0 %fusion.27 = f32[24,4,64,64]{3,0,1,2:T(8,128)} fusion(bf16[64,4,64,4,64]{4,3,2,1,0:T(4,128)(2,1)} %reshape_squeeze.3, bf16[64,4,24,64]{3,2,1,0:T(8,128)(2,1)S(1)} %reshape.152), kind=kOutput, calls=%fused_computation.45 | convolution fusion | flops 201326592 | bytes 10747904 | tf_op jit(solution)/shard_map/traw,apqrw->tpaq/dot_general | solution.py:81
  797.8 5.3 copy.32
  803.1 3.9 reshape.148
  (558 shorter events, 340.7 us)
Async XLA Ops:
  7.4 6.7 collective-permute-start
  18.7 5.7 collective-permute-start
  28.9 6.3 collective-permute-start
  39.6 6.4 collective-permute-start
  50.6 6.2 collective-permute-start
  61.2 6.4 collective-permute-start
  72.1 6.4 collective-permute-start
  82.9 6.4 collective-permute-start
  93.7 6.4 collective-permute-start
  104.5 6.4 collective-permute-start
  108.6 4.9 collective-permute-start.1
  115.8 5.9 collective-permute-start
  119.4 4.9 collective-permute-start.1
  126.6 6.3 collective-permute-start
  137.5 8.3 %collective-permute-start = (f32[1,4096]{1,0:T(1,128)S(1)}, f32[1,4096]{1,0:T(1,128)S(1)}, u32[]{:S(2)}, u32[]{:S(2)}) collective-permute-start(f32[1,4096]{1,0:T(1,128)S(1)} %get-tuple-element.446), channel_id=1, source_target_pairs={{0,1},{1,2},{2,3},{3,4},{4,5},{5,6},{6,7},{7,8},{8,9},{9,10},{10,1... | collective-permute-start | bytes 49160 | tf_op jit(solution)/shard_map/while/body/eval_jaxpr/ppermute | solution.py:16
  143.5 4.9 collective-permute-start.1
  150.7 8.1 collective-permute-start
  156.4 4.9 collective-permute-start.1
  163.6 8.1 collective-permute-start
  169.4 4.9 collective-permute-start.1
  176.6 8.1 collective-permute-start
  182.3 4.9 collective-permute-start.1
  189.5 8.1 collective-permute-start
  195.2 4.9 collective-permute-start.1
  202.4 8.1 collective-permute-start
  208.2 5.2 collective-permute-start.1
  215.7 7.8 collective-permute-start
  228.3 8.1 collective-permute-start
  241.1 8.2 %collective-permute-start = (f32[1,4096]{1,0:T(1,128)S(1)}, f32[1,4096]{1,0:T(1,128)S(1)}, u32[]{:S(2)}, u32[]{:S(2)}) collective-permute-start(f32[1,4096]{1,0:T(1,128)S(1)} %get-tuple-element.446), channel_id=1, source_target_pairs={{0,1},{1,2},{2,3},{3,4},{4,5},{5,6},{6,7},{7,8},{8,9},{9,10},{10,1... | collective-permute-start | bytes 49160 | tf_op jit(solution)/shard_map/while/body/eval_jaxpr/ppermute | solution.py:16
  253.8 8.5 %collective-permute-start = (f32[1,4096]{1,0:T(1,128)S(1)}, f32[1,4096]{1,0:T(1,128)S(1)}, u32[]{:S(2)}, u32[]{:S(2)}) collective-permute-start(f32[1,4096]{1,0:T(1,128)S(1)} %get-tuple-element.446), channel_id=1, source_target_pairs={{0,1},{1,2},{2,3},{3,4},{4,5},{5,6},{6,7},{7,8},{8,9},{9,10},{10,1... | collective-permute-start | bytes 49160 | tf_op jit(solution)/shard_map/while/body/eval_jaxpr/ppermute | solution.py:16
  267.0 8.2 %collective-permute-start = (f32[1,4096]{1,0:T(1,128)S(1)}, f32[1,4096]{1,0:T(1,128)S(1)}, u32[]{:S(2)}, u32[]{:S(2)}) collective-permute-start(f32[1,4096]{1,0:T(1,128)S(1)} %get-tuple-element.446), channel_id=1, source_target_pairs={{0,1},{1,2},{2,3},{3,4},{4,5},{5,6},{6,7},{7,8},{8,9},{9,10},{10,1... | collective-permute-start | bytes 49160 | tf_op jit(solution)/shard_map/while/body/eval_jaxpr/ppermute | solution.py:16
  279.6 8.5 %collective-permute-start = (f32[1,4096]{1,0:T(1,128)S(1)}, f32[1,4096]{1,0:T(1,128)S(1)}, u32[]{:S(2)}, u32[]{:S(2)}) collective-permute-start(f32[1,4096]{1,0:T(1,128)S(1)} %get-tuple-element.446), channel_id=1, source_target_pairs={{0,1},{1,2},{2,3},{3,4},{4,5},{5,6},{6,7},{7,8},{8,9},{9,10},{10,1... | collective-permute-start | bytes 49160 | tf_op jit(solution)/shard_map/while/body/eval_jaxpr/ppermute | solution.py:16
  298.3 31.7 %collective-permute-start.4 = (bf16[24,4,64,64]{3,0,1,2:T(8,128)(2,1)S(1)}, bf16[24,4,64,64]{3,0,1,2:T(8,128)(2,1)S(1)}, u32[]{:S(2)}, u32[]{:S(2)}) collective-permute-start(bf16[24,4,64,64]{3,0,1,2:T(8,128)(2,1)S(1)} %copy.14), channel_id=1, source_target_pairs={{0,64},{64,0},{1,65},{65,1},{2,66},{66,2},{3,67},{67,3},{4,68},{68... | collective-permute-start | bytes 2359304 | tf_op jit(solution)/shard_map/ppermute | solution.py:29
  334.9 61.4 %all-to-all-start = ((bf16[64,2,3072]{2,1,0:T(2,128)(2,1)}), bf16[64,2,3072]{2,1,0:T(2,128)(2,1)S(1)}, u32[]{:S(2)}, u32[]{:S(2)}) async-start(bf16[64,2,3072]{2,1,0:T(2,128)(2,1)} %reshape.149), calls=%async_computation | async-start | bytes 1572864 | tf_op jit(solution)/shard_map/all_to_all | solution.py:80
  422.3 5.1 collective-permute-start.2
  431.3 5.5 collective-permute-start.2
  440.6 7.0 collective-permute-start.2
  451.4 6.6 collective-permute-start.2
  461.9 6.2 collective-permute-start.2
  471.9 6.4 collective-permute-start.2
  482.1 6.4 collective-permute-start.2
  492.3 6.4 collective-permute-start.2
  502.6 6.4 collective-permute-start.2
  512.9 6.3 collective-permute-start.2
  523.1 6.3 collective-permute-start.2
  533.2 6.7 collective-permute-start.2
  543.8 8.2 %collective-permute-start.2 = (f32[1,4096]{1,0:T(1,128)S(1)}, f32[1,4096]{1,0:T(1,128)S(1)}, u32[]{:S(2)}, u32[]{:S(2)}) collective-permute-start(f32[1,4096]{1,0:T(1,128)S(1)} %get-tuple-element.463), channel_id=1, source_target_pairs={{0,1},{1,2},{2,3},{3,4},{4,5},{5,6},{6,7},{7,8},{8,9},{9,10},{10,1... | collective-permute-start | bytes 49160 | tf_op jit(solution)/shard_map/while/body/eval_jaxpr/ppermute | solution.py:16
  549.6 4.9 collective-permute-start.3
  556.2 8.1 %collective-permute-start.2 = (f32[1,4096]{1,0:T(1,128)S(1)}, f32[1,4096]{1,0:T(1,128)S(1)}, u32[]{:S(2)}, u32[]{:S(2)}) collective-permute-start(f32[1,4096]{1,0:T(1,128)S(1)} %get-tuple-element.463), channel_id=1, source_target_pairs={{0,1},{1,2},{2,3},{3,4},{4,5},{5,6},{6,7},{7,8},{8,9},{9,10},{10,1... | collective-permute-start | bytes 49160 | tf_op jit(solution)/shard_map/while/body/eval_jaxpr/ppermute | solution.py:16
  562.0 4.9 collective-permute-start.3
  568.5 8.1 %collective-permute-start.2 = (f32[1,4096]{1,0:T(1,128)S(1)}, f32[1,4096]{1,0:T(1,128)S(1)}, u32[]{:S(2)}, u32[]{:S(2)}) collective-permute-start(f32[1,4096]{1,0:T(1,128)S(1)} %get-tuple-element.463), channel_id=1, source_target_pairs={{0,1},{1,2},{2,3},{3,4},{4,5},{5,6},{6,7},{7,8},{8,9},{9,10},{10,1... | collective-permute-start | bytes 49160 | tf_op jit(solution)/shard_map/while/body/eval_jaxpr/ppermute | solution.py:16
  574.3 4.9 collective-permute-start.3
  580.9 8.1 %collective-permute-start.2 = (f32[1,4096]{1,0:T(1,128)S(1)}, f32[1,4096]{1,0:T(1,128)S(1)}, u32[]{:S(2)}, u32[]{:S(2)}) collective-permute-start(f32[1,4096]{1,0:T(1,128)S(1)} %get-tuple-element.463), channel_id=1, source_target_pairs={{0,1},{1,2},{2,3},{3,4},{4,5},{5,6},{6,7},{7,8},{8,9},{9,10},{10,1... | collective-permute-start | bytes 49160 | tf_op jit(solution)/shard_map/while/body/eval_jaxpr/ppermute | solution.py:16
  586.6 4.9 collective-permute-start.3
  593.2 8.1 %collective-permute-start.2 = (f32[1,4096]{1,0:T(1,128)S(1)}, f32[1,4096]{1,0:T(1,128)S(1)}, u32[]{:S(2)}, u32[]{:S(2)}) collective-permute-start(f32[1,4096]{1,0:T(1,128)S(1)} %get-tuple-element.463), channel_id=1, source_target_pairs={{0,1},{1,2},{2,3},{3,4},{4,5},{5,6},{6,7},{7,8},{8,9},{9,10},{10,1... | collective-permute-start | bytes 49160 | tf_op jit(solution)/shard_map/while/body/eval_jaxpr/ppermute | solution.py:16
  599.0 5.2 collective-permute-start.3
  605.9 7.8 collective-permute-start.2
  617.9 8.1 %collective-permute-start.2 = (f32[1,4096]{1,0:T(1,128)S(1)}, f32[1,4096]{1,0:T(1,128)S(1)}, u32[]{:S(2)}, u32[]{:S(2)}) collective-permute-start(f32[1,4096]{1,0:T(1,128)S(1)} %get-tuple-element.463), channel_id=1, source_target_pairs={{0,1},{1,2},{2,3},{3,4},{4,5},{5,6},{6,7},{7,8},{8,9},{9,10},{10,1... | collective-permute-start | bytes 49160 | tf_op jit(solution)/shard_map/while/body/eval_jaxpr/ppermute | solution.py:16
  630.1 8.2 %collective-permute-start.2 = (f32[1,4096]{1,0:T(1,128)S(1)}, f32[1,4096]{1,0:T(1,128)S(1)}, u32[]{:S(2)}, u32[]{:S(2)}) collective-permute-start(f32[1,4096]{1,0:T(1,128)S(1)} %get-tuple-element.463), channel_id=1, source_target_pairs={{0,1},{1,2},{2,3},{3,4},{4,5},{5,6},{6,7},{7,8},{8,9},{9,10},{10,1... | collective-permute-start | bytes 49160 | tf_op jit(solution)/shard_map/while/body/eval_jaxpr/ppermute | solution.py:16
  642.2 8.5 %collective-permute-start.2 = (f32[1,4096]{1,0:T(1,128)S(1)}, f32[1,4096]{1,0:T(1,128)S(1)}, u32[]{:S(2)}, u32[]{:S(2)}) collective-permute-start(f32[1,4096]{1,0:T(1,128)S(1)} %get-tuple-element.463), channel_id=1, source_target_pairs={{0,1},{1,2},{2,3},{3,4},{4,5},{5,6},{6,7},{7,8},{8,9},{9,10},{10,1... | collective-permute-start | bytes 49160 | tf_op jit(solution)/shard_map/while/body/eval_jaxpr/ppermute | solution.py:16
  654.8 8.2 %collective-permute-start.2 = (f32[1,4096]{1,0:T(1,128)S(1)}, f32[1,4096]{1,0:T(1,128)S(1)}, u32[]{:S(2)}, u32[]{:S(2)}) collective-permute-start(f32[1,4096]{1,0:T(1,128)S(1)} %get-tuple-element.463), channel_id=1, source_target_pairs={{0,1},{1,2},{2,3},{3,4},{4,5},{5,6},{6,7},{7,8},{8,9},{9,10},{10,1... | collective-permute-start | bytes 49160 | tf_op jit(solution)/shard_map/while/body/eval_jaxpr/ppermute | solution.py:16
  666.9 8.5 %collective-permute-start.2 = (f32[1,4096]{1,0:T(1,128)S(1)}, f32[1,4096]{1,0:T(1,128)S(1)}, u32[]{:S(2)}, u32[]{:S(2)}) collective-permute-start(f32[1,4096]{1,0:T(1,128)S(1)} %get-tuple-element.463), channel_id=1, source_target_pairs={{0,1},{1,2},{2,3},{3,4},{4,5},{5,6},{6,7},{7,8},{8,9},{9,10},{10,1... | collective-permute-start | bytes 49160 | tf_op jit(solution)/shard_map/while/body/eval_jaxpr/ppermute | solution.py:16
  679.2 8.9 %collective-permute-start.2 = (f32[1,4096]{1,0:T(1,128)S(1)}, f32[1,4096]{1,0:T(1,128)S(1)}, u32[]{:S(2)}, u32[]{:S(2)}) collective-permute-start(f32[1,4096]{1,0:T(1,128)S(1)} %get-tuple-element.463), channel_id=1, source_target_pairs={{0,1},{1,2},{2,3},{3,4},{4,5},{5,6},{6,7},{7,8},{8,9},{9,10},{10,1... | collective-permute-start | bytes 49160 | tf_op jit(solution)/shard_map/while/body/eval_jaxpr/ppermute | solution.py:16
  696.8 32.1 %collective-permute-start.5 = (bf16[24,4,64,64]{3,0,1,2:T(8,128)(2,1)S(1)}, bf16[24,4,64,64]{3,0,1,2:T(8,128)(2,1)S(1)}, u32[]{:S(2)}, u32[]{:S(2)}) collective-permute-start(bf16[24,4,64,64]{3,0,1,2:T(8,128)(2,1)S(1)} %copy.19), channel_id=1, source_target_pairs={{0,64},{64,0},{1,65},{65,1},{2,66},{66,2},{3,67},{67,3},{4,68},{68... | collective-permute-start | bytes 2359304 | tf_op jit(solution)/shard_map/ppermute | solution.py:29
  (43 other events, 181.8 us)
where the time goes:
time: 815 us; the launch traced here: 807 us
  starting transfers between devices  391 us (48%)
  other arithmetic  136 us (17%)
  waiting for transfers between devices  118 us (14%)
  local copies, waits for them, and re-layouts  78.6 us (10%)
  blocking collectives  51.1 us (6%)
  matrix products  28.5 us (3%)
    ppermute x48, starting transfers between devices, padded_2(): before = lax.ppermute(last, axis, up)  234 us
    ppermute x48, waiting for transfers between devices, padded_2(): after = lax.ppermute(initial, axis, down)  112 us
    dynamic_update_slice x48, other arithmetic, on_device(): column, trace = lax.scan(one_step, state[0], forcing)  93.2 us
    ppermute x48, starting transfers between devices, padded_2(): after = lax.ppermute(initial, axis, down)  62 us
    ppermute x2, starting transfers between devices, from_partner(): return lax.ppermute(block, axis, route)  57.7 us
    all_to_all x1, blocking collectives, on_device(): lax.all_to_all(partner, 'tile', split_axis=2, concat_axis=2, tiled=True)  51.1 us
    all_to_all x1, starting transfers between devices, on_device(): lax.all_to_all(partner, 'tile', split_axis=2, concat_axis=2, tiled=True)  36.9 us
    dot_general x2, matrix products, on_device(): jnp.einsum('traw,apqrw->tpaq', arrived, blocks, preferred_element_type=jn...  28.5 us
  transfers between devices with their start and end apart: 99, of which 50 were waited for; matrix products, arithmetic and copies ran while one was open for 9% of the time, Pallas kernels for 0%

commit v1 on v0

v1 whole, which is shorter than its diff:
```python
import functools

import jax
import jax.numpy as jnp
from jax import lax
from jax.experimental import pallas as pl
from jax.experimental.pallas import tpu as pltpu
from jax.sharding import PartitionSpec as P

MESH = pl.DeviceIdType.MESH
F32 = jnp.float32
BF16 = jnp.bfloat16
K = 4
CHUNK = 8
ITERS = 2


def kernel(
    dims,
    state, guess, regrid, regime, land, land_temp, rates, vertical, mixing,
    final, forcing,
    us, force, wts, cx, raw, land_scale, land_add, own, hs, hr, q, sf, snd, rcv, gf,
    in_sem, coef_send, coef_recv, halo_send, halo_recv, trace_send, trace_recv, out_sem,
):
    tiles, levels, steps, size, regimes = dims
    macros = steps // K
    chunks = steps // CHUNK
    total = ITERS * macros
    last = ITERS * chunks - 1
    member = lax.axis_index("mp")
    tile = lax.axis_index("tile")
    has_up, has_down = tile > 0, tile < tiles - 1

    row = lax.broadcasted_iota(jnp.int32, (size, 128), 0)
    lane = lax.broadcasted_iota(jnp.int32, (size, 128), 1)
    strip_row = row % K

    small = [
        pltpu.make_async_copy(regime, raw.at[0], in_sem.at[0]),
        pltpu.make_async_copy(land, raw.at[1], in_sem.at[1]),
        pltpu.make_async_copy(land_temp, land_add, in_sem.at[2]),
    ]
    load_state = pltpu.make_async_copy(state, us.at[0], in_sem.at[3])
    load_guess = pltpu.make_async_copy(guess, force.at[pl.ds(0, steps)], in_sem.at[4])
    load_weights = pltpu.make_async_copy(regrid, wts, in_sem.at[5])
    for copy in small:
        copy.start()
    load_state.start()
    load_guess.start()
    load_weights.start()

    barrier = pltpu.get_barrier_semaphore()

    def greet(o, _):
        pl.semaphore_signal(barrier, inc=1, device_id=(1 - member, o), device_id_type=MESH)
        return 0

    lax.fori_loop(0, tiles, greet, 0)

    @pl.when(has_up)
    def _():
        pl.semaphore_signal(barrier, inc=1, device_id=(member, tile - 1), device_id_type=MESH)

    @pl.when(has_down)
    def _():
        pl.semaphore_signal(barrier, inc=1, device_id=(member, tile + 1), device_id_type=MESH)

    def clear(side):
        cx[2 * side] = jnp.zeros((size, 128), F32)

        def one(m, _):
            hr[m, side] = jnp.zeros((3, size, 128), BF16)
            return 0

        lax.fori_loop(0, total, one, 0)

    pl.when(jnp.logical_not(has_up))(lambda: clear(0))
    pl.when(jnp.logical_not(has_down))(lambda: clear(1))

    mix = mixing[0]
    mix_up = jnp.where(has_up, mix, 0.0)
    mix_down = jnp.where(has_down, mix, 0.0)
    vert = [vertical[0, l] for l in range(levels - 1)]

    for copy in small:
        copy.wait()
    kind = raw[0]
    coeff = jnp.zeros((size, 128), F32)
    for index in range(regimes):
        coeff = coeff + jnp.where(kind == index, rates[0, index], 0.0)
    is_land = raw[1] == 1
    cx[1] = coeff
    land_scale[...] = jnp.where(is_land, 0.0, coeff)
    land_add[...] = jnp.where(is_land, coeff * land_add[...], 0.0)

    def coef_copies():
        up = pltpu.make_async_remote_copy(
            cx.at[1], cx.at[2], coef_send.at[0], coef_recv.at[1], device_id=(member, tile - 1), device_id_type=MESH
        )
        down = pltpu.make_async_remote_copy(
            cx.at[1], cx.at[0], coef_send.at[1], coef_recv.at[0], device_id=(member, tile + 1), device_id_type=MESH
        )
        return up, down

    def halo_copies(m):
        up = pltpu.make_async_remote_copy(
            hs.at[m, pl.ds(0, 3)], hr.at[m, 1], halo_send.at[m, 0], halo_recv.at[m, 1],
            device_id=(member, tile - 1), device_id_type=MESH,
        )
        down = pltpu.make_async_remote_copy(
            hs.at[m, pl.ds(1, 3)], hr.at[m, 0], halo_send.at[m, 1], halo_recv.at[m, 0],
            device_id=(member, tile + 1), device_id_type=MESH,
        )
        return up, down

    def start(copies):
        up, down = copies
        pl.when(has_up)(lambda: up.start())
        pl.when(has_down)(lambda: down.start())

    def wait_recv(copies):
        up, down = copies
        pl.when(has_up)(lambda: down.wait_recv())
        pl.when(has_down)(lambda: up.wait_recv())

    def wait_send(copies):
        up, down = copies
        pl.when(has_up)(lambda: up.wait_send())
        pl.when(has_down)(lambda: down.wait_send())

    def advance(cols, count, c, source):
        between = [vert[l] * (cols[l + 1] - cols[l]) for l in range(min(count, levels - 1))]
        new = [cols[0] + between[0] + (source - c * cols[0])]
        for l in range(1, count):
            if l < levels - 1:
                new.append(cols[l] + between[l] - between[l - 1])
            else:
                new.append(cols[l] - between[l - 1])
        return new

    def responses(m, source, ahead):
        slot = m % 2
        srow = lax.broadcasted_iota(jnp.int32, (16, 128), 0) % K

        def one(p, _):
            rows = pl.ds(pl.multiple_of(p * 16, 16), 16)
            depth = 2 * K if ahead else K
            cols = [us[source, l, rows, :] for l in range(depth)]
            c = cx[1, rows, :]
            if ahead:
                for i in range(K):
                    cols = advance(cols, depth - 1 - i, c, q[i, rows, :])
            scale, add = land_scale[rows, :], land_add[rows, :]
            free = [cols[0]]
            for i in range(K - 1):
                cols = advance(cols, K - 1 - i, c, add + scale * force[K * m + i, rows, :])
                free.append(cols[0])
            for i in range(K):
                own[slot, i, rows, :] = free[i]
            hs[m, 0, rows, :] = jnp.where(srow == K - 1, pltpu.roll(free[3], 3, 0), free[1]).astype(BF16)
            hs[m, 1, rows, :] = free[0].astype(BF16)
            hs[m, 2, rows, :] = free[2].astype(BF16)
            hs[m, 3, rows, :] = jnp.where(srow == 0, pltpu.roll(free[3], 13, 0), free[1]).astype(BF16)
            return 0

        lax.fori_loop(0, size // 16, one, 0)

    def across(x):
        left = pltpu.roll(jnp.where(lane == 127, pltpu.roll(x, K, 0), x), 1, 1)
        right = pltpu.roll(jnp.where(lane == 0, pltpu.roll(x, size - K, 0), x), 127, 1)
        return left + right - 4.0 * x

    def simulate(m):
        slot = m % 2
        up_mid = hr[m, 0, 2].astype(F32)
        down_mid = hr[m, 1, 0].astype(F32)
        up_free = [hr[m, 0, 0].astype(F32), up_mid, hr[m, 0, 1].astype(F32), pltpu.roll(up_mid, 3, 0)]
        down_free = [hr[m, 1, 1].astype(F32), down_mid, hr[m, 1, 2].astype(F32), pltpu.roll(down_mid, size - 3, 0)]
        v0 = vert[0]
        gain = [1.0 - v0 - cx[k] for k in range(3)]
        mixes = (mix_up, mix, mix_down)
        up, mid, down = up_free[0], own[slot, 0], down_free[0]
        first = [None] * 3
        second = [None] * 3
        for i in range(K):
            above = jnp.where(strip_row == 0, pltpu.roll(up, size - 3, 0), pltpu.roll(mid, 1, 0))
            below = jnp.where(strip_row == K - 1, pltpu.roll(down, 3, 0), pltpu.roll(mid, size - 1, 0))
            sides = [None, mix * (above + below + across(mid)), None]
            q[i] = land_add[...] + land_scale[...] * force[K * m + i] + sides[1]
            if i == K - 1:
                break
            up_below = jnp.where(strip_row == K - 1, pltpu.roll(mid, 3, 0), pltpu.roll(up, size - 1, 0))
            down_above = jnp.where(strip_row == 0, pltpu.roll(mid, size - 3, 0), pltpu.roll(down, 1, 0))
            sides[0] = mix_up * (pltpu.roll(up, 1, 0) + up_below + across(up))
            sides[2] = mix_down * (pltpu.roll(down, size - 1, 0) + down_above + across(down))
            for k in range(3):
                response = sides[k]
                if first[k] is not None:
                    response = response + gain[k] * first[k]
                if second[k] is not None:
                    response = response + v0 * second[k]
                second[k] = None if first[k] is None else v0 * first[k]
                first[k] = response
            up = up_free[i + 1] + first[0]
            mid = own[slot, i + 1] + first[1]
            down = down_free[i + 1] + first[2]

    def swap(x):
        r = lax.broadcasted_iota(jnp.int32, x.shape, 0) % 2
        high = lax.broadcasted_iota(jnp.int32, x.shape, 1) >= 64
        other = pltpu.roll(x, 64, 1)
        n = x.shape[0]
        moved = jnp.where(r == 1, pltpu.roll(other, 1, 0), pltpu.roll(other, n - 1, 0))
        return jnp.where((r == 1) == high, x, moved)

    def columns(m, source):
        at = (m % 2) * K

        def one(p, _):
            rows = pl.ds(pl.multiple_of(p * 8, 8), 8)
            cols = [us[source, l, rows, :] for l in range(levels)]
            c = cx[1, rows, :]
            for i in range(K):
                cols = advance(cols, levels, c, q[i, rows, :])
                sf[pl.ds(p * 64 + at + i, 8, stride=8), :] = swap(cols[0])
            for l in range(levels):
                us[1, l, rows, :] = cols[l]
            return 0

        lax.fori_loop(0, size // 8, one, 0)

    def trace_copy(g, o):
        return pltpu.make_async_remote_copy(
            snd.at[g, o], rcv.at[g, tile], trace_send.at[g], trace_recv.at[g],
            device_id=(1 - member, o), device_id_type=MESH,
        )

    def whole_trace(g):
        return pltpu.make_async_remote_copy(
            snd.at[g], rcv.at[g], trace_send.at[g], trace_recv.at[g], device_id=(1 - member, tile), device_id_type=MESH
        )

    def send_trace(g):
        def pack(j, _):
            for h in range(2):
                low = sf[pl.ds(pl.multiple_of((j * 4 + h) * 8, 8), 8), :]
                high = sf[pl.ds(pl.multiple_of((j * 4 + 2 + h) * 8, 8), 8), :]
                snd[g, 2 * j + h] = jnp.concatenate([low, high], axis=0).astype(BF16)
            return 0

        lax.fori_loop(0, tiles // 2, pack, 0)

        def send(k, _):
            trace_copy(g, lax.rem(tile + k, tiles)).start()
            return 0

        lax.fori_loop(0, tiles, send, 0)

    def product(g, begin, count):
        def one(j, _):
            for h in range(2):
                a = 2 * j + h
                block = rcv[g, a]
                cells = jnp.concatenate([block[:8], block[8:]], axis=1)
                out = lax.dot_general(cells, wts[a], (((1,), (1,)), ((), ())), preferred_element_type=F32)
                gf[pl.ds(pl.multiple_of((j * 4 + h) * 8, 8), 8), :] = out[:, :128]
                gf[pl.ds(pl.multiple_of((j * 4 + 2 + h) * 8, 8), 8), :] = out[:, 128:]
            return 0

        lax.fori_loop(begin // 2, (begin + count) // 2, one, 0)

    def spread(g):
        def one(t, _):
            force[steps + g * CHUNK + t] = swap(gf[pl.ds(t, size, stride=8), :])
            return 0

        lax.fori_loop(0, CHUNK, one, 0)

    def put(g):
        part = g - (ITERS - 1) * chunks
        return pltpu.make_async_copy(
            force.at[pl.ds(steps + g * CHUNK, CHUNK)], forcing.at[pl.ds(part * CHUNK, CHUNK)], out_sem.at[part]
        )

    load_state.wait()
    load_guess.wait()
    responses(0, 0, False)
    pl.semaphore_wait(barrier, tiles + jnp.where(has_up, 1, 0) + jnp.where(has_down, 1, 0))
    start(coef_copies())
    start(halo_copies(0))
    wait_recv(coef_copies())

    def macro(m, _):
        within = lax.rem(m, macros)
        source = jnp.minimum(within, 1)
        odd = lax.rem(m, 2) == 1
        wait_recv(halo_copies(m))
        simulate(m)

        @pl.when(within < macros - 1)
        def _():
            responses(m + 1, source, True)
            start(halo_copies(m + 1))

        columns(m, source)

        @pl.when(odd)
        def _():
            send_trace(m // 2)

        @pl.when(m == 3)
        def _():
            load_weights.wait()

        @pl.when(jnp.logical_and(odd, m >= 3))
        def _():
            g = (m - 3) // 2
            whole_trace(g).wait_recv()
            product(g, 0, tiles // 2)

        @pl.when(jnp.logical_and(jnp.logical_not(odd), m >= 4))
        def _():
            g = (m - 4) // 2
            product(g, tiles // 2, tiles // 2)
            spread(g)

        @pl.when(m == 4)
        def _():
            responses(macros, 0, False)
            start(halo_copies(macros))

        return 0

    lax.fori_loop(0, total, macro, 0)

    put_final = pltpu.make_async_copy(us.at[1], final, out_sem.at[chunks])
    put_final.start()
    put(last - 2).start()
    product(last - 1, tiles // 2, tiles // 2)
    spread(last - 1)
    put(last - 1).start()
    whole_trace(last).wait_recv()
    product(last, 0, tiles)
    spread(last)
    put(last).start()

    wait_send(coef_copies())

    def drain(m, _):
        wait_send(halo_copies(m))
        return 0

    lax.fori_loop(0, total, drain, 0)

    def drain_trace(g, _):
        whole_trace(g).wait_send()
        return 0

    lax.fori_loop(0, last + 1, drain_trace, 0)
    put_final.wait()
    for g in range(last - 2, last + 1):
        put(g).wait()


def to_tiles(x):
    n, rows, width = x.shape
    return x.reshape(n, rows, width // 128, 128).transpose(0, 2, 1, 3).reshape(n, rows * width // 128, 128)


def from_tiles(x, rows):
    n, size, _ = x.shape
    return x.reshape(n, size // rows, rows, 128).transpose(0, 2, 1, 3).reshape(n, rows, size // rows * 128)


def on_device(state, guess, regrid, regime, land, land_temp, exchange_rate, vertical, mixing):
    levels, rows, width = state.shape[1:]
    steps = guess.shape[1]
    tiles = lax.axis_size("tile")
    size = rows * width // 128
    cells = regrid.shape[-1]
    macros = ITERS * steps // K
    groups = ITERS * steps // CHUNK
    dims = (tiles, levels, steps, size, exchange_rate.shape[1])
    hbm = pl.BlockSpec(memory_space=pl.ANY)
    smem = pl.BlockSpec(memory_space=pltpu.SMEM)
    dma = pltpu.SemaphoreType.DMA
    final, forcing = pl.pallas_call(
        functools.partial(kernel, dims),
        out_shape=(
            jax.ShapeDtypeStruct((levels, size, 128), F32),
            jax.ShapeDtypeStruct((steps, size, 128), F32),
        ),
        in_specs=[hbm] * 6 + [smem] * 3,
        out_specs=(hbm, hbm),
        scratch_shapes=[
            pltpu.VMEM((2, levels, size, 128), F32),
            pltpu.VMEM(((ITERS + 1) * steps, size, 128), F32),
            pltpu.VMEM((tiles, cells, cells), BF16),
            pltpu.VMEM((3, size, 128), F32),
            pltpu.VMEM((2, size, 128), jnp.int32),
            pltpu.VMEM((size, 128), F32),
            pltpu.VMEM((size, 128), F32),
            pltpu.VMEM((2, K, size, 128), F32),
            pltpu.VMEM((macros, 4, size, 128), BF16),
            pltpu.VMEM((macros, 2, 3, size, 128), BF16),
            pltpu.VMEM((K, size, 128), F32),
            pltpu.VMEM((8 * size, 128), F32),
            pltpu.VMEM((groups, tiles, 16, 128), BF16),
            pltpu.VMEM((groups, tiles, 16, 128), BF16),
            pltpu.VMEM((8 * size, 128), F32),
            dma((6,)),
            dma((2,)),
            dma((2,)),
            dma((macros, 2)),
            dma((macros, 2)),
            dma((groups,)),
            dma((groups,)),
            dma((groups // ITERS + 1,)),
        ],
        compiler_params=pltpu.CompilerParams(
            collective_id=0, has_side_effects=True, vmem_limit_bytes=60 * 1024 * 1024
        ),
    )(
        to_tiles(state[0]),
        to_tiles(guess[0]),
        regrid[0, 0],
        to_tiles(regime)[0],
        to_tiles(land)[0],
        to_tiles(land_temp)[0],
        exchange_rate,
        vertical,
        mixing,
    )
    return from_tiles(final, rows)[None], from_tiles(forcing, rows)[None]


def solution(mesh):
    return jax.shard_map(
        on_device,
        mesh=mesh,
        in_specs=(
            P("mp", None, "tile", None),
            P("mp", None, "tile", None),
            P("mp", "tile", None, None, None),
            P("mp", "tile", None),
            P("mp", "tile", None),
            P("mp", "tile", None),
            P("mp", None),
            P("mp", None),
            P("mp"),
        ),
        out_specs=(P("mp", None, "tile", None), P("mp", None, "tile", None)),
        check_vma=False,
    )
```

time: 815 us -> 121 us (0.15)
  starting transfers between devices: 391 us -> 0 us
  other arithmetic: 136 us -> 0 us
  waiting for transfers between devices: 118 us -> 0 us
  Pallas kernels: 0 us -> 115 us
  local copies, waits for them, and re-layouts: 78.6 us -> 3.76 us
  blocking collectives: 51.1 us -> 0 us
  matrix products: 28.5 us -> 0 us
    ppermute x98 -> x0, starting transfers between devices: 354 us -> none  [the longest x48 234 us: padded_2(): before = lax.ppermute(last, axis, up)]
    ppermute x98 -> x0, waiting for transfers between devices: 118 us -> none  [the longest x48 112 us: padded_2(): after = lax.ppermute(initial, axis, down)]
    pallas_call x0 -> x1, Pallas kernels: none -> 115 us  [on_device(): pl.pallas_call(functools.partial(kernel, dims), out_shape=(jax.ShapeDtype...]
    dynamic_update_slice x48 -> x0, other arithmetic: 93.2 us -> none  [on_device(): column, trace = lax.scan(one_step, state[0], forcing)]
    all_to_all x1 -> x0, blocking collectives: 51.1 us -> none  [on_device(): lax.all_to_all(partner, 'tile', split_axis=2, concat_axis=2, tiled=True)]
    all_to_all x1 -> x0, starting transfers between devices: 36.9 us -> none  [on_device(): lax.all_to_all(partner, 'tile', split_axis=2, concat_axis=2, tiled=True)]
    dot_general x2 -> x0, matrix products: 28.5 us -> none  [on_device(): jnp.einsum('traw,apqrw->tpaq', arrived, blocks, preferred_element_type=jn...]
    another operation x3 -> x0, local copies, waits for them, and re-layouts: 26.1 us -> none  [the longest x1 24.5 us: on_device(): blocks = regrid[0, 0].reshape(tiles, rows, face, rows, face)]
  transfers between devices with their start and end apart: 99 -> 0, of which waited for: 50 -> 0; matrix products, arithmetic and copies ran while one was open for 9% -> 0% of each run, Pallas kernels for 0% -> 0%
where the time goes in v1:
time: 121 us; the launch traced here: 120 us
  Pallas kernels  115 us (95%)
  local copies, waits for them, and re-layouts  3.76 us (3%)
  between operations  1.3 us (1%)
    pallas_call x1, Pallas kernels, on_device(): pl.pallas_call(functools.partial(kernel, dims), out_shape=(jax.ShapeDtype...  115 us
    unnamed x4, local copies, waits for them, and re-layouts  3.76 us

profile of v1, /device:TPU:1, one launch (start us, length us, event | category | flops | bytes accessed | tf_op | source)
XLA Modules:
  0.0 119.9 jit_solution(3780390068301223589)
XLA Ops:
  1.3 114.9 %shard_map.104 = (f32[20,128,128]{2,1,0:T(8,128)}, f32[24,128,128]{2,1,0:T(8,128)}) custom-call(f32[20,128,128]{2,1,0:T(8,128)} %bitcast.39, f32[24,128,128]{2,1,0:T(8,128)} %bitcast.37, bf16[64,256,256]{2,1,0:T(8,128)(2,1)} %bitcast.36, s32[128,128]{1,0:T(8,128)} %bitcast.41, s32[128,128]{1,0:T(8,128)} %bitcast.42, f32[128,128]{1,0:T(8,128)} %bitcast.43, ...), custom_call_target="tpu_custom_call" | custom-call | tf_op jit(solution)/shard_map/pallas_call | solution.py:387
  116.2 0.0 copy-start
  116.2 2.6 %copy.21 = f32[1,20,4,4096]{3,2,1,0:T(4,128)} copy(f32[1,20,4,4096]{3,2,1,0:T(4,128)} %bitcast.40) | data formatting | bytes 2621440
  118.8 0.0 copy-done
  118.8 1.1 copy.22
Async XLA Ops:
  116.2 2.6 %copy-start = (f32[24,128,128]{2,1,0:T(8,128)S(1)}, f32[24,128,128]{2,1,0:T(8,128)}, u32[]{:S(2)}) copy-start(f32[24,128,128]{2,1,0:T(8,128)} %get-tuple-element.5) | copy-start | bytes 4718596

commit v2 on v1

--- a/solution.py
+++ b/solution.py
@@ -13,13 +13,14 @@
 K = 4
 CHUNK = 8
 ITERS = 2
+UNROLL = 4
 
 
 def kernel(
     dims,
     state, guess, regrid, regime, land, land_temp, rates, vertical, mixing,
     final, forcing,
-    us, force, wts, cx, raw, land_scale, land_add, own, hs, hr, q, sf, snd, rcv, gf,
+    us, force, wts, cx, raw, land_scale, land_add, own, hs0, hs1, hs2, hr0, hr1, hr2, q, tr, sf, snd, rcv, gf,
     in_sem, coef_send, coef_recv, halo_send, halo_recv, trace_send, trace_recv, out_sem,
 ):
     tiles, levels, steps, size, regimes = dims
@@ -40,14 +41,19 @@
         pltpu.make_async_copy(land, raw.at[1], in_sem.at[1]),
         pltpu.make_async_copy(land_temp, land_add, in_sem.at[2]),
     ]
-    load_state = pltpu.make_async_copy(state, us.at[0], in_sem.at[3])
-    load_guess = pltpu.make_async_copy(guess, force.at[pl.ds(0, steps)], in_sem.at[4])
-    load_weights = pltpu.make_async_copy(regrid, wts, in_sem.at[5])
-    for copy in small:
+    def load_state(begin, count, sem):
+        part = pl.ds(begin, count)
+        return pltpu.make_async_copy(state.at[part], us.at[0, part], in_sem.at[sem])
+
+    def load_guess(begin, count, sem):
+        part = pl.ds(begin, count)
+        return pltpu.make_async_copy(guess.at[part], force.at[part], in_sem.at[sem])
+
+    early = [load_state(0, K, 3), load_guess(0, K, 4)]
+    late = [load_state(K, levels - K, 5), load_guess(K, steps - K, 6)]
+    load_weights = pltpu.make_async_copy(regrid, wts, in_sem.at[7])
+    for copy in small + early + late:
         copy.start()
-    load_state.start()
-    load_guess.start()
-    load_weights.start()
 
     barrier = pltpu.get_barrier_semaphore()
 
@@ -69,7 +75,9 @@
         cx[2 * side] = jnp.zeros((size, 128), F32)
 
         def one(m, _):
-            hr[m, side] = jnp.zeros((3, size, 128), BF16)
+            hr0[m, side] = jnp.zeros((size, 128), BF16)
+            hr1[m, side] = jnp.zeros((size, 128), BF16)
+            hr2[m, side] = jnp.zeros((size // 2, 128), BF16)
             return 0
 
         lax.fori_loop(0, total, one, 0)
@@ -102,13 +110,15 @@
         )
         return up, down
 
-    def halo_copies(m):
+    def halo_copies(m, part):
+        sources = (hs0.at[m], hs0.at[m]), (hs1.at[m, 0], hs1.at[m, 1]), (hs2.at[m, 0], hs2.at[m, 1])
+        target = (hr0, hr1, hr2)[part]
         up = pltpu.make_async_remote_copy(
-            hs.at[m, pl.ds(0, 3)], hr.at[m, 1], halo_send.at[m, 0], halo_recv.at[m, 1],
+            sources[part][0], target.at[m, 1], halo_send.at[m, part, 0], halo_recv.at[m, part, 1],
             device_id=(member, tile - 1), device_id_type=MESH,
         )
         down = pltpu.make_async_remote_copy(
-            hs.at[m, pl.ds(1, 3)], hr.at[m, 0], halo_send.at[m, 1], halo_recv.at[m, 0],
+            sources[part][1], target.at[m, 0], halo_send.at[m, part, 1], halo_recv.at[m, part, 0],
             device_id=(member, tile + 1), device_id_type=MESH,
         )
         return up, down
@@ -157,13 +167,20 @@
                 free.append(cols[0])
             for i in range(K):
                 own[slot, i, rows, :] = free[i]
-            hs[m, 0, rows, :] = jnp.where(srow == K - 1, pltpu.roll(free[3], 3, 0), free[1]).astype(BF16)
-            hs[m, 1, rows, :] = free[0].astype(BF16)
-            hs[m, 2, rows, :] = free[2].astype(BF16)
-            hs[m, 3, rows, :] = jnp.where(srow == 0, pltpu.roll(free[3], 13, 0), free[1]).astype(BF16)
+            hs0[m, rows, :] = free[0].astype(BF16)
+            hs1[m, 0, rows, :] = jnp.where(srow == K - 1, pltpu.roll(free[3], 3, 0), free[1]).astype(BF16)
+            hs1[m, 1, rows, :] = jnp.where(srow == 0, pltpu.roll(free[3], 13, 0), free[1]).astype(BF16)
             return 0
 
         lax.fori_loop(0, size // 16, one, 0)
+        start(halo_copies(m, 0))
+        start(halo_copies(m, 1))
+        half = size // 2
+        near, far = own[slot, 2, :half, :], own[slot, 2, half:, :]
+        upper = strip_row[:half] < 2
+        hs2[m, 0] = jnp.where(upper, near, pltpu.roll(far, 2, 0)).astype(BF16)
+        hs2[m, 1] = jnp.where(upper, pltpu.roll(far, half - 2, 0), near).astype(BF16)
+        start(halo_copies(m, 2))
 
     def across(x):
         left = pltpu.roll(jnp.where(lane == 127, pltpu.roll(x, K, 0), x), 1, 1)
@@ -172,38 +189,72 @@
 
     def simulate(m):
         slot = m % 2
-        up_mid = hr[m, 0, 2].astype(F32)
-        down_mid = hr[m, 1, 0].astype(F32)
-        up_free = [hr[m, 0, 0].astype(F32), up_mid, hr[m, 0, 1].astype(F32), pltpu.roll(up_mid, 3, 0)]
-        down_free = [hr[m, 1, 1].astype(F32), down_mid, hr[m, 1, 2].astype(F32), pltpu.roll(down_mid, size - 3, 0)]
         v0 = vert[0]
-        gain = [1.0 - v0 - cx[k] for k in range(3)]
-        mixes = (mix_up, mix, mix_down)
-        up, mid, down = up_free[0], own[slot, 0], down_free[0]
-        first = [None] * 3
-        second = [None] * 3
-        for i in range(K):
-            above = jnp.where(strip_row == 0, pltpu.roll(up, size - 3, 0), pltpu.roll(mid, 1, 0))
-            below = jnp.where(strip_row == K - 1, pltpu.roll(down, 3, 0), pltpu.roll(mid, size - 1, 0))
-            sides = [None, mix * (above + below + across(mid)), None]
-            q[i] = land_add[...] + land_scale[...] * force[K * m + i] + sides[1]
-            if i == K - 1:
-                break
-            up_below = jnp.where(strip_row == K - 1, pltpu.roll(mid, 3, 0), pltpu.roll(up, size - 1, 0))
-            down_above = jnp.where(strip_row == 0, pltpu.roll(mid, size - 3, 0), pltpu.roll(down, 1, 0))
-            sides[0] = mix_up * (pltpu.roll(up, 1, 0) + up_below + across(up))
-            sides[2] = mix_down * (pltpu.roll(down, size - 1, 0) + down_above + across(down))
-            for k in range(3):
-                response = sides[k]
-                if first[k] is not None:
-                    response = response + gain[k] * first[k]
-                if second[k] is not None:
-                    response = response + v0 * second[k]
-                second[k] = None if first[k] is None else v0 * first[k]
-                first[k] = response
-            up = up_free[i + 1] + first[0]
-            mid = own[slot, i + 1] + first[1]
-            down = down_free[i + 1] + first[2]
+
+        def source(i, lateral):
+            q[i] = land_add[...] + land_scale[...] * force[K * m + i] + mix * lateral
+
+        def shifted(mid):
+            return pltpu.roll(mid, size - 3, 0), pltpu.roll(mid, 3, 0)
+
+        top, bottom = strip_row == 0, strip_row == K - 1
+        wait_recv(halo_copies(m, 0))
+        up, mid, down = hr0[m, 0].astype(F32), own[slot, 0], hr0[m, 1].astype(F32)
+        last_mid, first_mid = shifted(mid)
+        above = jnp.where(top, pltpu.roll(up, size - 3, 0), pltpu.roll(mid, 1, 0))
+        below = jnp.where(bottom, pltpu.roll(down, 3, 0), pltpu.roll(mid, size - 1, 0))
+        lateral = above + below + across(mid)
+        source(0, lateral)
+        mid_w = mix * lateral
+        below = jnp.where(bottom, first_mid, pltpu.roll(up, size - 1, 0))
+        up_w = mix_up * (pltpu.roll(up, 1, 0) + below + across(up))
+        above = jnp.where(top, last_mid, pltpu.roll(down, 1, 0))
+        down_w = mix_down * (above + pltpu.roll(down, size - 1, 0) + across(down))
+        wait_recv(halo_copies(m, 1))
+        from_up = strip_row >= 2
+        up_free, down_free = hr1[m, 0].astype(F32), hr1[m, 1].astype(F32)
+        up, mid, down = up_free + up_w, own[slot, 1] + mid_w, down_free + down_w
+        edge_mix = jnp.where(from_up, mix_up, mix_down)
+        edge_gain = 1.0 - v0 - jnp.where(from_up, cx[0], cx[2])
+        mid_gain = 1.0 - v0 - cx[1]
+        edge = jnp.where(from_up, up, down)
+        edge_w = jnp.where(from_up, up_w, down_w)
+        last_mid, first_mid = shifted(mid)
+        above = jnp.where(top, pltpu.roll(up, size - 3, 0), pltpu.roll(mid, 1, 0))
+        below = jnp.where(bottom, pltpu.roll(down, 3, 0), pltpu.roll(mid, size - 1, 0))
+        lateral = above + below + across(mid)
+        source(1, lateral)
+        mid_next = mid_gain * mid_w + mix * lateral
+        above = jnp.where(top, last_mid, pltpu.roll(jnp.where(top, down, up), 1, 0))
+        below = jnp.where(bottom, first_mid, pltpu.roll(jnp.where(bottom, up, down), size - 1, 0))
+        edge_next = edge_gain * edge_w + edge_mix * (above + below + across(edge))
+        wait_recv(halo_copies(m, 2))
+        half = size // 2
+        up_free2, down_free2 = hr2[m, 0].astype(F32), hr2[m, 1].astype(F32)
+        low = from_up[:half]
+        free = jnp.concatenate(
+            [
+                jnp.where(low, up_free2, down_free2),
+                jnp.where(low, pltpu.roll(up_free2, 2, 0), pltpu.roll(down_free2, half - 2, 0)),
+            ],
+            axis=0,
+        )
+        mid, edge = own[slot, 2] + mid_next, free + edge_next
+        last_mid, first_mid = shifted(mid)
+
+        def middle(mid, edge):
+            above = jnp.where(top, pltpu.roll(edge, size - 3, 0), pltpu.roll(mid, 1, 0))
+            below = jnp.where(bottom, pltpu.roll(edge, 3, 0), pltpu.roll(mid, size - 1, 0))
+            return above + below + across(mid)
+
+        lateral = middle(mid, edge)
+        source(2, lateral)
+        mid_w = mid_gain * mid_next + v0 * v0 * mid_w + mix * lateral
+        above = jnp.where(top, last_mid, pltpu.roll(edge, 1, 0))
+        below = jnp.where(bottom, first_mid, pltpu.roll(edge, size - 1, 0))
+        edge_w = edge_gain * edge_next + v0 * v0 * edge_w + edge_mix * (above + below + across(edge))
+        free = jnp.where(from_up, pltpu.roll(up_free, 3, 0), pltpu.roll(down_free, size - 3, 0))
+        source(3, middle(own[slot, 3] + mid_w, free + edge_w))
 
     def swap(x):
         r = lax.broadcasted_iota(jnp.int32, x.shape, 0) % 2
@@ -222,12 +273,14 @@
             c = cx[1, rows, :]
             for i in range(K):
                 cols = advance(cols, levels, c, q[i, rows, :])
-                sf[pl.ds(p * 64 + at + i, 8, stride=8), :] = swap(cols[0])
+                tr[i, rows, :] = cols[0]
             for l in range(levels):
                 us[1, l, rows, :] = cols[l]
             return 0
 
         lax.fori_loop(0, size // 8, one, 0)
+        for i in range(K):
+            sf[pl.ds(at + i, size, stride=8), :] = swap(tr[i])
 
     def trace_copy(g, o):
         return pltpu.make_async_remote_copy(
@@ -240,7 +293,7 @@
             snd.at[g], rcv.at[g], trace_send.at[g], trace_recv.at[g], device_id=(1 - member, tile), device_id_type=MESH
         )
 
-    def send_trace(g):
+    def pack_trace(g):
         def pack(j, _):
             for h in range(2):
                 low = sf[pl.ds(pl.multiple_of((j * 4 + h) * 8, 8), 8), :]
@@ -248,13 +301,14 @@
                 snd[g, 2 * j + h] = jnp.concatenate([low, high], axis=0).astype(BF16)
             return 0
 
-        lax.fori_loop(0, tiles // 2, pack, 0)
-
+        lax.fori_loop(0, tiles // 2, pack, 0, unroll=4)
+
+    def send_trace(g, begin, end):
         def send(k, _):
             trace_copy(g, lax.rem(tile + k, tiles)).start()
             return 0
 
-        lax.fori_loop(0, tiles, send, 0)
+        lax.fori_loop(begin, end, send, 0)
 
     def product(g, begin, count):
         def one(j, _):
@@ -267,7 +321,7 @@
                 gf[pl.ds(pl.multiple_of((j * 4 + 2 + h) * 8, 8), 8), :] = out[:, 128:]
             return 0
 
-        lax.fori_loop(begin // 2, (begin + count) // 2, one, 0)
+        lax.fori_loop(begin // 2, (begin + count) // 2, one, 0, unroll=UNROLL)
 
     def spread(g):
         def one(t, _):
@@ -282,31 +336,36 @@
             force.at[pl.ds(steps + g * CHUNK, CHUNK)], forcing.at[pl.ds(part * CHUNK, CHUNK)], out_sem.at[part]
         )
 
-    load_state.wait()
-    load_guess.wait()
+    for copy in early:
+        copy.wait()
+    pl.semaphore_wait(barrier, tiles + jnp.where(has_up, 1, 0) + jnp.where(has_down, 1, 0))
     responses(0, 0, False)
-    pl.semaphore_wait(barrier, tiles + jnp.where(has_up, 1, 0) + jnp.where(has_down, 1, 0))
     start(coef_copies())
-    start(halo_copies(0))
+    for copy in late:
+        copy.wait()
+    load_weights.start()
     wait_recv(coef_copies())
 
     def macro(m, _):
         within = lax.rem(m, macros)
         source = jnp.minimum(within, 1)
         odd = lax.rem(m, 2) == 1
-        wait_recv(halo_copies(m))
         simulate(m)
 
         @pl.when(within < macros - 1)
         def _():
             responses(m + 1, source, True)
-            start(halo_copies(m + 1))
+
+        @pl.when(jnp.logical_and(jnp.logical_not(odd), m >= 2))
+        def _():
+            send_trace(m // 2 - 1, tiles // 2, tiles)
 
         columns(m, source)
 
         @pl.when(odd)
         def _():
-            send_trace(m // 2)
+            pack_trace(m // 2)
+            send_trace(m // 2, 0, jnp.where(m == total - 1, tiles, tiles // 2))
 
         @pl.when(m == 3)
         def _():
@@ -327,7 +386,6 @@
         @pl.when(m == 4)
         def _():
             responses(macros, 0, False)
-            start(halo_copies(macros))
 
         return 0
 
@@ -347,7 +405,8 @@
     wait_send(coef_copies())
 
     def drain(m, _):
-        wait_send(halo_copies(m))
+        for part in range(3):
+            wait_send(halo_copies(m, part))
         return 0
 
     lax.fori_loop(0, total, drain, 0)
@@ -401,18 +460,23 @@
             pltpu.VMEM((size, 128), F32),
             pltpu.VMEM((size, 128), F32),
             pltpu.VMEM((2, K, size, 128), F32),
-            pltpu.VMEM((macros, 4, size, 128), BF16),
-            pltpu.VMEM((macros, 2, 3, size, 128), BF16),
+            pltpu.VMEM((macros, size, 128), BF16),
+            pltpu.VMEM((macros, 2, size, 128), BF16),
+            pltpu.VMEM((macros, 2, size // 2, 128), BF16),
+            pltpu.VMEM((macros, 2, size, 128), BF16),
+            pltpu.VMEM((macros, 2, size, 128), BF16),
+            pltpu.VMEM((macros, 2, size // 2, 128), BF16),
+            pltpu.VMEM((K, size, 128), F32),
             pltpu.VMEM((K, size, 128), F32),
             pltpu.VMEM((8 * size, 128), F32),
             pltpu.VMEM((groups, tiles, 16, 128), BF16),
             pltpu.VMEM((groups, tiles, 16, 128), BF16),
             pltpu.VMEM((8 * size, 128), F32),
-            dma((6,)),
+            dma((8,)),
             dma((2,)),
             dma((2,)),
-            dma((macros, 2)),
-            dma((macros, 2)),
+            dma((macros, 3, 2)),
+            dma((macros, 3, 2)),
             dma((groups,)),
             dma((groups,)),
             dma((groups // ITERS + 1,)),

time: 121 us -> 109 us (0.901)
  Pallas kernels: 115 us -> 104 us
    pallas_call x1, Pallas kernels: 115 us -> 104 us  [on_device(): pl.pallas_call(functools.partial(kernel, dims), out_shape=(jax.ShapeDtype...]
where the time goes in v2:
time: 109 us
  Pallas kernels  104 us (95%)
  local copies, waits for them, and re-layouts  3.76 us (3%)
  between operations  1.3 us (1%)
    pallas_call x1, Pallas kernels, on_device(): pl.pallas_call(functools.partial(kernel, dims), out_shape=(jax.ShapeDtype...  104 us
    unnamed x4, local copies, waits for them, and re-layouts  3.76 us

profile of v2, /device:TPU:1, one launch (start us, length us, event | category | flops | bytes accessed | tf_op | source)
XLA Modules:
  0.0 108.9 jit_solution(18289507524000859723)
XLA Ops:
  1.3 103.8 %shard_map.104 = (f32[20,128,128]{2,1,0:T(8,128)}, f32[24,128,128]{2,1,0:T(8,128)}) custom-call(f32[20,128,128]{2,1,0:T(8,128)} %bitcast.39, f32[24,128,128]{2,1,0:T(8,128)} %bitcast.37, bf16[64,256,256]{2,1,0:T(8,128)(2,1)} %bitcast.36, s32[128,128]{1,0:T(8,128)} %bitcast.41, s32[128,128]{1,0:T(8,128)} %bitcast.42, f32[128,128]{1,0:T(8,128)} %bitcast.43, ...), custom_call_target="tpu_custom_call" | custom-call | tf_op jit(solution)/shard_map/pallas_call | solution.py:446
  105.1 0.0 copy-start
  105.1 2.6 %copy.21 = f32[1,20,4,4096]{3,2,1,0:T(4,128)} copy(f32[1,20,4,4096]{3,2,1,0:T(4,128)} %bitcast.40) | data formatting | bytes 2621440
  107.8 0.0 copy-done
  107.8 1.1 %copy.22 = f32[1,24,4,4096]{3,2,1,0:T(4,128)} copy(f32[1,24,4,4096]{3,2,1,0:T(4,128)S(1)} %bitcast.38) | data formatting | bytes 3145728
Async XLA Ops:
  105.1 2.6 %copy-start = (f32[24,128,128]{2,1,0:T(8,128)S(1)}, f32[24,128,128]{2,1,0:T(8,128)}, u32[]{:S(2)}) copy-start(f32[24,128,128]{2,1,0:T(8,128)} %get-tuple-element.5) | copy-start | bytes 4718596

commit v3 on v1

v3 whole, which is shorter than its diff:
```python
import functools

import jax
import jax.numpy as jnp
from jax import lax
from jax.experimental import pallas as pl
from jax.experimental.pallas import tpu as pltpu
from jax.sharding import PartitionSpec as P

MESH = pl.DeviceIdType.MESH
F32 = jnp.float32
BF16 = jnp.bfloat16
K = 4
CHUNK = 8
ITERS = 2
UNROLL = 4
LAG = 4


def kernel(
    dims,
    state, guess, regrid, regime, land, land_temp, rates_in, vertical_in, mixing,
    final, forcing,
    rates, vertical, us, force, wts, cx, raw, land_scale, land_add, own, hs, hr, q, tr, sf, snd, rcv, gf,
    in_sem, coef_send, coef_recv, halo_send, halo_recv, trace_send, trace_recv, out_sem,
):
    tiles, levels, steps, size, regimes = dims
    macros = steps // K
    chunks = steps // CHUNK
    total = ITERS * macros
    slots = macros + LAG * (ITERS - 1)
    last = ITERS * chunks - 1
    member = lax.axis_index("mp")
    tile = lax.axis_index("tile")
    has_up, has_down = tile > 0, tile < tiles - 1

    row = lax.broadcasted_iota(jnp.int32, (size, 128), 0)
    lane = lax.broadcasted_iota(jnp.int32, (size, 128), 1)
    strip_row = row % K

    small = [
        pltpu.make_async_copy(regime, raw.at[0], in_sem.at[0]),
        pltpu.make_async_copy(land, raw.at[1], in_sem.at[1]),
        pltpu.make_async_copy(land_temp, land_add, in_sem.at[2]),
        pltpu.make_async_copy(rates_in, rates, in_sem.at[8]),
        pltpu.make_async_copy(vertical_in, vertical, in_sem.at[9]),
    ]
    def load_state(begin, count, sem):
        part = pl.ds(begin, count)
        return pltpu.make_async_copy(state.at[part], us.at[0, part], in_sem.at[sem])

    def load_guess(begin, count, sem):
        part = pl.ds(begin, count)
        return pltpu.make_async_copy(guess.at[part], force.at[part], in_sem.at[sem])

    early = [load_state(0, K, 3), load_guess(0, K, 4)]
    late = [load_state(K, levels - K, 5), load_guess(K, steps - K, 6)]
    load_weights = pltpu.make_async_copy(regrid, wts, in_sem.at[7])
    for copy in small + early + late:
        copy.start()

    barrier = pltpu.get_barrier_semaphore()

    def greet(o, _):
        pl.semaphore_signal(barrier, inc=1, device_id=(1 - member, o), device_id_type=MESH)
        return 0

    lax.fori_loop(0, tiles, greet, 0, unroll=4)

    @pl.when(has_up)
    def _():
        pl.semaphore_signal(barrier, inc=1, device_id=(member, tile - 1), device_id_type=MESH)

    @pl.when(has_down)
    def _():
        pl.semaphore_signal(barrier, inc=1, device_id=(member, tile + 1), device_id_type=MESH)

    def clear(side):
        cx[2 * side] = jnp.zeros((size, 128), F32)

        def one(m, _):
            hr[m, side] = jnp.zeros((size, 128), BF16)
            return 0

        lax.fori_loop(0, total, one, 0)

    pl.when(jnp.logical_not(has_up))(lambda: clear(0))
    pl.when(jnp.logical_not(has_down))(lambda: clear(1))

    for copy in small:
        copy.wait()
    mix = mixing[0]
    mix_up = jnp.where(has_up, mix, 0.0)
    mix_down = jnp.where(has_down, mix, 0.0)
    vert = [vertical[0, l] for l in range(levels - 1)]

    kind = raw[0]
    coeff = jnp.zeros((size, 128), F32)
    for index in range(regimes):
        coeff = coeff + jnp.where(kind == index, rates[0, index], 0.0)
    is_land = raw[1] == 1
    cx[1] = coeff
    land_scale[...] = jnp.where(is_land, 0.0, coeff)
    land_add[...] = jnp.where(is_land, coeff * land_add[...], 0.0)

    def coef_copies():
        up = pltpu.make_async_remote_copy(
            cx.at[1], cx.at[2], coef_send.at[0], coef_recv.at[1], device_id=(member, tile - 1), device_id_type=MESH
        )
        down = pltpu.make_async_remote_copy(
            cx.at[1], cx.at[0], coef_send.at[1], coef_recv.at[0], device_id=(member, tile + 1), device_id_type=MESH
        )
        return up, down

    def halo_copies(m):
        up = pltpu.make_async_remote_copy(
            hs.at[m, 0], hr.at[m, 1], halo_send.at[m, 0], halo_recv.at[m, 1],
            device_id=(member, tile - 1), device_id_type=MESH,
        )
        down = pltpu.make_async_remote_copy(
            hs.at[m, 1], hr.at[m, 0], halo_send.at[m, 1], halo_recv.at[m, 0],
            device_id=(member, tile + 1), device_id_type=MESH,
        )
        return up, down

    def start(copies):
        up, down = copies
        pl.when(has_up)(lambda: up.start())
        pl.when(has_down)(lambda: down.start())

    def wait_recv(copies):
        up, down = copies
        pl.when(has_up)(lambda: down.wait_recv())
        pl.when(has_down)(lambda: up.wait_recv())

    def wait_send(copies):
        up, down = copies
        pl.when(has_up)(lambda: up.wait_send())
        pl.when(has_down)(lambda: down.wait_send())

    def advance(cols, count, c, source):
        between = [vert[l] * (cols[l + 1] - cols[l]) for l in range(min(count, levels - 1))]
        new = [cols[0] + between[0] + (source - c * cols[0])]
        for l in range(1, count):
            if l < levels - 1:
                new.append(cols[l] + between[l] - between[l - 1])
            else:
                new.append(cols[l] - between[l - 1])
        return new

    top, bottom, from_up = strip_row == 0, strip_row == K - 1, strip_row >= 2

    def across(x):
        left = pltpu.roll(jnp.where(lane == 127, pltpu.roll(x, K, 0), x), 1, 1)
        right = pltpu.roll(jnp.where(lane == 0, pltpu.roll(x, size - K, 0), x), 127, 1)
        return left + right - 4.0 * x

    def turn(x, shift):
        return x if shift == 0 else pltpu.roll(x, shift % size, 0)

    def responses(m, window, source, ahead, send=True):
        slot = m % 4

        def one(p, _):
            rows = pl.ds(pl.multiple_of(p * 16, 16), 16)
            depth = 2 * K if ahead else K
            cols = [us[source, l, rows, :] for l in range(depth)]
            c = cx[1, rows, :]
            if ahead:
                for i in range(K):
                    cols = advance(cols, depth - 1 - i, c, q[window, i, rows, :])
            scale, add = land_scale[rows, :], land_add[rows, :]
            own[slot, 0, rows, :] = cols[0]
            for i in range(K - 1):
                cols = advance(cols, K - 1 - i, c, add + scale * force[K * m + i, rows, :])
                own[slot, i + 1, rows, :] = cols[0]
            return 0

        lax.fori_loop(0, size // 16, one, 0)

        def closed(x):
            above = jnp.where(top, 0.0, pltpu.roll(x, 1, 0))
            below = jnp.where(bottom, 0.0, pltpu.roll(x, size - 1, 0))
            return mix * (above + below + across(x))

        v0 = vert[0]
        gain = 1.0 - v0 - cx[1]
        ends = [own[slot, 0]]
        first = closed(ends[0])
        ends.append(own[slot, 1] + first)
        second = gain * first + closed(ends[1])
        ends.append(own[slot, 2] + second)
        ends.append(own[slot, 3] + gain * second + v0 * v0 * first + closed(ends[2]))
        to_up, to_down = ends[0], turn(ends[0], -3)
        for i in range(1, K):
            to_up = jnp.where(strip_row == i, turn(ends[i], i), to_up)
            to_down = jnp.where(strip_row == i, turn(ends[i], i - 3), to_down)
        hs[m, 0] = to_up.astype(BF16)
        hs[m, 1] = to_down.astype(BF16)
        if send:
            start(halo_copies(m))

    def simulate(m, window):
        slot = m % 4
        v0 = vert[0]
        gain = 1.0 - v0 - cx[1]
        edge_mix = jnp.where(from_up, mix_up, mix_down)
        edge_gain = 1.0 - v0 - jnp.where(from_up, cx[0], cx[2])
        wait_recv(halo_copies(m))
        up, down = hr[m, 0].astype(F32), hr[m, 1].astype(F32)

        def lateral(i, mid, edge):
            before, after = turn(up, -i), turn(down, 3 - i)
            if edge is not None:
                before, after = before + turn(edge, -3), after + turn(edge, 3)
            above = jnp.where(top, before, pltpu.roll(mid, 1, 0))
            below = jnp.where(bottom, after, pltpu.roll(mid, size - 1, 0))
            out = mix * (above + below + across(mid))
            q[window, i] = land_add[...] + land_scale[...] * force[K * m + i] + out
            return out

        def beyond(mid, edge):
            above = jnp.where(top, turn(mid, -3), pltpu.roll(edge, 1, 0))
            below = jnp.where(bottom, turn(mid, 3), pltpu.roll(edge, size - 1, 0))
            return edge_mix * (above + below + across(edge))

        mid = own[slot, 0]
        mid_1 = lateral(0, mid, None)
        edge_1 = edge_mix * jnp.where(top, turn(mid, -3), jnp.where(bottom, turn(mid, 3), 0.0))
        mid = own[slot, 1] + mid_1
        mid_2 = gain * mid_1 + lateral(1, mid, edge_1)
        edge_2 = edge_gain * edge_1 + beyond(mid, edge_1)
        mid = own[slot, 2] + mid_2
        mid_3 = gain * mid_2 + v0 * v0 * mid_1 + lateral(2, mid, edge_2)
        edge_3 = edge_gain * edge_2 + v0 * v0 * edge_1 + beyond(mid, edge_2)
        lateral(3, own[slot, 3] + mid_3, edge_3)

    def swap(x):
        r = lax.broadcasted_iota(jnp.int32, x.shape, 0) % 2
        high = lax.broadcasted_iota(jnp.int32, x.shape, 1) >= 64
        other = pltpu.roll(x, 64, 1)
        n = x.shape[0]
        moved = jnp.where(r == 1, pltpu.roll(other, 1, 0), pltpu.roll(other, n - 1, 0))
        return jnp.where((r == 1) == high, x, moved)

    def columns(m, window, source, depth, keep, trace=True):
        at = (m % 2) * K

        def one(p, _):
            rows = pl.ds(pl.multiple_of(p * 8, 8), 8)
            cols = [us[source, l, rows, :] for l in range(depth)]
            c = cx[1, rows, :]
            for i in range(K):
                cols = advance(cols, levels if depth == levels else depth - 1 - i, c, q[window, i, rows, :])
                if trace:
                    tr[i, rows, :] = cols[0]
            for l in range(keep):
                us[1 + window, l, rows, :] = cols[l]
            return 0

        lax.fori_loop(0, size // 8, one, 0)
        if trace:
            for i in range(K):
                sf[window, pl.ds(at + i, size, stride=8), :] = swap(tr[i])

    def trace_copy(g, o):
        return pltpu.make_async_remote_copy(
            snd.at[g, o], rcv.at[g, tile], trace_send.at[g], trace_recv.at[g],
            device_id=(1 - member, o), device_id_type=MESH,
        )

    def whole_trace(g):
        return pltpu.make_async_remote_copy(
            snd.at[g], rcv.at[g], trace_send.at[g], trace_recv.at[g], device_id=(1 - member, tile), device_id_type=MESH
        )

    def send_trace(g, window):
        def pack(j, _):
            for h in range(2):
                low = sf[window, pl.ds(pl.multiple_of((j * 4 + h) * 8, 8), 8), :]
                high = sf[window, pl.ds(pl.multiple_of((j * 4 + 2 + h) * 8, 8), 8), :]
                snd[g, 2 * j + h] = jnp.concatenate([low, high], axis=0).astype(BF16)
            return 0

        lax.fori_loop(0, tiles // 2, pack, 0, unroll=4)

        def send(k, _):
            trace_copy(g, lax.rem(tile + k, tiles)).start()
            return 0

        lax.fori_loop(0, tiles, send, 0, unroll=4)

    def product(g, begin, count):
        def one(j, _):
            for h in range(2):
                a = 2 * j + h
                block = rcv[g, a]
                cells = jnp.concatenate([block[:8], block[8:]], axis=1)
                out = lax.dot_general(cells, wts[a], (((1,), (1,)), ((), ())), preferred_element_type=F32)
                gf[pl.ds(pl.multiple_of((j * 4 + h) * 8, 8), 8), :] = out[:, :128]
                gf[pl.ds(pl.multiple_of((j * 4 + 2 + h) * 8, 8), 8), :] = out[:, 128:]
            return 0

        lax.fori_loop(begin // 2, (begin + count) // 2, one, 0, unroll=UNROLL)

    def spread(g):
        def one(t, _):
            force[steps + g * CHUNK + t] = swap(gf[pl.ds(t, size, stride=8), :])
            return 0

        lax.fori_loop(0, CHUNK, one, 0)

    def put(g):
        part = g - (ITERS - 1) * chunks
        return pltpu.make_async_copy(
            force.at[pl.ds(steps + g * CHUNK, CHUNK)], forcing.at[pl.ds(part * CHUNK, CHUNK)], out_sem.at[part]
        )

    for copy in early:
        copy.wait()
    responses(0, 0, 0, False, False)
    pl.semaphore_wait(barrier, tiles + jnp.where(has_up, 1, 0) + jnp.where(has_down, 1, 0))
    start(halo_copies(0))
    start(coef_copies())
    for copy in late:
        copy.wait()
    load_weights.start()
    wait_recv(coef_copies())

    def group(s, _):
        def members(body):
            def one(window, _):
                within = s - LAG * window

                @pl.when(jnp.logical_and(within >= 0, within < macros))
                def _():
                    body(window, within, macros * window + within, jnp.where(within == 0, 0, 1 + window))

                return 0

            lax.fori_loop(0, ITERS, one, 0)

        def surface(window, within, m, source):
            simulate(m, window)

            @pl.when(within < macros - 1)
            def _():
                responses(m + 1, window, source, True)

        def depth(window, within, m, source):
            end = window == ITERS - 1
            full = jnp.logical_or(within < macros - 2, jnp.logical_and(end, within < macros - 1))

            @pl.when(full)
            def _():
                columns(m, window, source, levels, levels)

            @pl.when(jnp.logical_and(jnp.logical_not(end), within == macros - 2))
            def _():
                columns(m, window, source, 2 * K + 1, K + 1)

            @pl.when(within == macros - 1)
            def _():
                columns(m, window, source, K + 1, 0)

            @pl.when(lax.rem(m, 2) == 1)
            def _():
                send_trace(m // 2, window)

            @pl.when(m == total - 1)
            def _():
                columns(m, window, source, levels, levels, False)

        members(surface)
        members(depth)

        @pl.when(s == LAG - 1)
        def _():
            load_weights.wait()

        @pl.when(jnp.logical_and(s >= LAG - 1, jnp.logical_and(s != LAG + 1, s < LAG + 1 + last - 1)))
        def _():
            g = jnp.where(s <= LAG, s - (LAG - 1), s - LAG)
            whole_trace(g).wait_recv()
            product(g, 0, tiles)
            spread(g)

        @pl.when(s == LAG - 1)
        def _():
            responses(macros, 1, 0, False)

        return 0

    lax.fori_loop(0, slots, group, 0)

    put_final = pltpu.make_async_copy(us.at[ITERS], final, out_sem.at[chunks])
    put_final.start()
    put(last - 2).start()
    put(last - 1).start()
    whole_trace(last).wait_recv()
    product(last, 0, tiles)
    spread(last)
    put(last).start()

    wait_send(coef_copies())

    def drain(m, _):
        wait_send(halo_copies(m))
        return 0

    lax.fori_loop(0, total, drain, 0)

    def drain_trace(g, _):
        whole_trace(g).wait_send()
        return 0

    lax.fori_loop(0, last + 1, drain_trace, 0)
    put_final.wait()
    for g in range(last - 2, last + 1):
        put(g).wait()


def to_tiles(x):
    n, rows, width = x.shape
    return x.reshape(n, rows, width // 128, 128).transpose(0, 2, 1, 3).reshape(n, rows * width // 128, 128)


def from_tiles(x, rows):
    n, size, _ = x.shape
    return x.reshape(n, size // rows, rows, 128).transpose(0, 2, 1, 3).reshape(n, rows, size // rows * 128)


def on_device(state, guess, regrid, regime, land, land_temp, exchange_rate, vertical, mixing):
    levels, rows, width = state.shape[1:]
    steps = guess.shape[1]
    tiles = lax.axis_size("tile")
    size = rows * width // 128
    cells = regrid.shape[-1]
    macros = ITERS * steps // K
    groups = ITERS * steps // CHUNK
    dims = (tiles, levels, steps, size, exchange_rate.shape[1])
    hbm = pl.BlockSpec(memory_space=pl.ANY)
    dma = pltpu.SemaphoreType.DMA
    final, forcing = pl.pallas_call(
        functools.partial(kernel, dims),
        out_shape=(
            jax.ShapeDtypeStruct((levels, size, 128), F32),
            jax.ShapeDtypeStruct((steps, size, 128), F32),
        ),
        in_specs=[hbm] * 8 + [pl.BlockSpec(memory_space=pltpu.SMEM)],
        out_specs=(hbm, hbm),
        scratch_shapes=[
            pltpu.SMEM(exchange_rate.shape, F32),
            pltpu.SMEM(vertical.shape, F32),
            pltpu.VMEM((1 + ITERS, levels, size, 128), F32),
            pltpu.VMEM(((ITERS + 1) * steps, size, 128), F32),
            pltpu.VMEM((tiles, cells, cells), BF16),
            pltpu.VMEM((3, size, 128), F32),
            pltpu.VMEM((2, size, 128), jnp.int32),
            pltpu.VMEM((size, 128), F32),
            pltpu.VMEM((size, 128), F32),
            pltpu.VMEM((4, K, size, 128), F32),
            pltpu.VMEM((macros, 2, size, 128), BF16),
            pltpu.VMEM((macros, 2, size, 128), BF16),
            pltpu.VMEM((ITERS, K, size, 128), F32),
            pltpu.VMEM((K, size, 128), F32),
            pltpu.VMEM((ITERS, 8 * size, 128), F32),
            pltpu.VMEM((groups, tiles, 16, 128), BF16),
            pltpu.VMEM((groups, tiles, 16, 128), BF16),
            pltpu.VMEM((8 * size, 128), F32),
            dma((10,)),
            dma((2,)),
            dma((2,)),
            dma((macros, 2)),
            dma((macros, 2)),
            dma((groups,)),
            dma((groups,)),
            dma((groups // ITERS + 1,)),
        ],
        compiler_params=pltpu.CompilerParams(
            collective_id=0, has_side_effects=True, vmem_limit_bytes=60 * 1024 * 1024
        ),
    )(
        to_tiles(state[0]),
        to_tiles(guess[0]),
        regrid[0, 0],
        to_tiles(regime)[0],
        to_tiles(land)[0],
        to_tiles(land_temp)[0],
        exchange_rate,
        vertical,
        mixing,
    )
    return from_tiles(final, rows)[None], from_tiles(forcing, rows)[None]


def solution(mesh):
    return jax.shard_map(
        on_device,
        mesh=mesh,
        in_specs=(
            P("mp", None, "tile", None),
            P("mp", None, "tile", None),
            P("mp", "tile", None, None, None),
            P("mp", "tile", None),
            P("mp", "tile", None),
            P("mp", "tile", None),
            P("mp", None),
            P("mp", None),
            P("mp"),
        ),
        out_specs=(P("mp", None, "tile", None), P("mp", None, "tile", None)),
        check_vma=False,
    )
```

time: 121 us -> 101 us (0.83)
  Pallas kernels: 115 us -> 95.5 us
    pallas_call x1, Pallas kernels: 115 us -> 95.5 us  [on_device(): pl.pallas_call(functools.partial(kernel, dims), out_shape=(jax.ShapeDtype...]
where the time goes in v3:
time: 101 us
  Pallas kernels  95.5 us (95%)
  local copies, waits for them, and re-layouts  3.76 us (4%)
  between operations  1.3 us (1%)
    pallas_call x1, Pallas kernels, on_device(): pl.pallas_call(functools.partial(kernel, dims), out_shape=(jax.ShapeDtype...  95.5 us
    unnamed x4, local copies, waits for them, and re-layouts  3.76 us

profile of v3, /device:TPU:1, one launch (start us, length us, event | category | flops | bytes accessed | tf_op | source)
XLA Modules:
  0.0 100.6 jit_solution(10346030323611703144)
XLA Ops:
  1.3 95.5 %shard_map.104 = (f32[20,128,128]{2,1,0:T(8,128)}, f32[24,128,128]{2,1,0:T(8,128)}) custom-call(f32[20,128,128]{2,1,0:T(8,128)} %bitcast.39, f32[24,128,128]{2,1,0:T(8,128)} %bitcast.37, bf16[64,256,256]{2,1,0:T(8,128)(2,1)} %bitcast.36, s32[128,128]{1,0:T(8,128)} %bitcast.41, s32[128,128]{1,0:T(8,128)} %bitcast.42, f32[128,128]{1,0:T(8,128)} %bitcast.43, ...), custom_call_target="tpu_custom_call" | custom-call | tf_op jit(solution)/shard_map/pallas_call | solution.py:444
  96.8 0.0 copy-start
  96.8 2.6 %copy.21 = f32[1,20,4,4096]{3,2,1,0:T(4,128)} copy(f32[1,20,4,4096]{3,2,1,0:T(4,128)} %bitcast.40) | data formatting | bytes 2621440
  99.4 0.0 copy-done
  99.4 1.1 %copy.22 = f32[1,24,4,4096]{3,2,1,0:T(4,128)} copy(f32[1,24,4,4096]{3,2,1,0:T(4,128)S(1)} %bitcast.38) | data formatting | bytes 3145728
Async XLA Ops:
  96.8 2.6 %copy-start = (f32[24,128,128]{2,1,0:T(8,128)S(1)}, f32[24,128,128]{2,1,0:T(8,128)}, u32[]{:S(2)}) copy-start(f32[24,128,128]{2,1,0:T(8,128)} %get-tuple-element.5) | copy-start | bytes 4718596

commit v4 on v3

--- a/solution.py
+++ b/solution.py
@@ -13,7 +13,7 @@
 K = 4
 CHUNK = 8
 ITERS = 2
-UNROLL = 4
+UNROLL = 8
 LAG = 4
 
 
@@ -176,7 +176,7 @@
                 own[slot, i + 1, rows, :] = cols[0]
             return 0
 
-        lax.fori_loop(0, size // 16, one, 0)
+        lax.fori_loop(0, size // 16, one, 0, unroll=2)
 
         def closed(x):
             above = jnp.where(top, 0.0, pltpu.roll(x, 1, 0))
@@ -187,6 +187,7 @@
         gain = 1.0 - v0 - cx[1]
         ends = [own[slot, 0]]
         first = closed(ends[0])
+        own[slot, K] = first
         ends.append(own[slot, 1] + first)
         second = gain * first + closed(ends[1])
         ends.append(own[slot, 2] + second)
@@ -206,33 +207,38 @@
         gain = 1.0 - v0 - cx[1]
         edge_mix = jnp.where(from_up, mix_up, mix_down)
         edge_gain = 1.0 - v0 - jnp.where(from_up, cx[0], cx[2])
+        mid = own[slot, 0]
+        inside = jnp.where(top, turn(mid, -3), jnp.where(bottom, turn(mid, 3), 0.0))
+        edge_1 = edge_mix * inside
+        edge_ahead = (
+            jnp.where(top, 0.0, pltpu.roll(edge_1, 1, 0))
+            + jnp.where(bottom, 0.0, pltpu.roll(edge_1, size - 1, 0))
+            + across(edge_1)
+        )
+        for i in range(K):
+            q[window, i] = land_add[...] + land_scale[...] * force[K * m + i]
         wait_recv(halo_copies(m))
         up, down = hr[m, 0].astype(F32), hr[m, 1].astype(F32)
 
         def lateral(i, mid, edge):
-            before, after = turn(up, -i), turn(down, 3 - i)
-            if edge is not None:
-                before, after = before + turn(edge, -3), after + turn(edge, 3)
+            before, after = turn(up, -i) + turn(edge, -3), turn(down, 3 - i) + turn(edge, 3)
             above = jnp.where(top, before, pltpu.roll(mid, 1, 0))
             below = jnp.where(bottom, after, pltpu.roll(mid, size - 1, 0))
             out = mix * (above + below + across(mid))
-            q[window, i] = land_add[...] + land_scale[...] * force[K * m + i] + out
+            q[window, i] += out
             return out
 
-        def beyond(mid, edge):
-            above = jnp.where(top, turn(mid, -3), pltpu.roll(edge, 1, 0))
-            below = jnp.where(bottom, turn(mid, 3), pltpu.roll(edge, size - 1, 0))
-            return edge_mix * (above + below + across(edge))
-
-        mid = own[slot, 0]
-        mid_1 = lateral(0, mid, None)
-        edge_1 = edge_mix * jnp.where(top, turn(mid, -3), jnp.where(bottom, turn(mid, 3), 0.0))
+        mid_1 = own[slot, K] + mix * jnp.where(top, up, jnp.where(bottom, turn(down, 3), 0.0))
+        q[window, 0] += mid_1
         mid = own[slot, 1] + mid_1
+        inside = jnp.where(top, turn(mid, -3), jnp.where(bottom, turn(mid, 3), 0.0))
+        edge_2 = edge_gain * edge_1 + edge_mix * (edge_ahead + inside)
         mid_2 = gain * mid_1 + lateral(1, mid, edge_1)
-        edge_2 = edge_gain * edge_1 + beyond(mid, edge_1)
         mid = own[slot, 2] + mid_2
+        above = jnp.where(top, turn(mid, -3), pltpu.roll(edge_2, 1, 0))
+        below = jnp.where(bottom, turn(mid, 3), pltpu.roll(edge_2, size - 1, 0))
+        edge_3 = edge_gain * edge_2 + v0 * v0 * edge_1 + edge_mix * (above + below + across(edge_2))
         mid_3 = gain * mid_2 + v0 * v0 * mid_1 + lateral(2, mid, edge_2)
-        edge_3 = edge_gain * edge_2 + v0 * v0 * edge_1 + beyond(mid, edge_2)
         lateral(3, own[slot, 3] + mid_3, edge_3)
 
     def swap(x):
@@ -258,7 +264,7 @@
                 us[1 + window, l, rows, :] = cols[l]
             return 0
 
-        lax.fori_loop(0, size // 8, one, 0)
+        lax.fori_loop(0, size // 8, one, 0, unroll=2)
         if trace:
             for i in range(K):
                 sf[window, pl.ds(at + i, size, stride=8), :] = swap(tr[i])
@@ -378,9 +384,9 @@
         def _():
             load_weights.wait()
 
-        @pl.when(jnp.logical_and(s >= LAG - 1, jnp.logical_and(s != LAG + 1, s < LAG + 1 + last - 1)))
+        @pl.when(jnp.logical_or(s == LAG - 1, jnp.logical_and(s >= LAG, lax.rem(s - LAG, 2) == 0)))
         def _():
-            g = jnp.where(s <= LAG, s - (LAG - 1), s - LAG)
+            g = jnp.where(s < LAG, 0, (s - LAG) // 2 + 1)
             whole_trace(g).wait_recv()
             product(g, 0, tiles)
             spread(g)
@@ -396,6 +402,9 @@
     put_final = pltpu.make_async_copy(us.at[ITERS], final, out_sem.at[chunks])
     put_final.start()
     put(last - 2).start()
+    whole_trace(last - 1).wait_recv()
+    product(last - 1, 0, tiles)
+    spread(last - 1)
     put(last - 1).start()
     whole_trace(last).wait_recv()
     product(last, 0, tiles)
@@ -459,7 +468,7 @@
             pltpu.VMEM((2, size, 128), jnp.int32),
             pltpu.VMEM((size, 128), F32),
             pltpu.VMEM((size, 128), F32),
-            pltpu.VMEM((4, K, size, 128), F32),
+            pltpu.VMEM((4, K + 1, size, 128), F32),
             pltpu.VMEM((macros, 2, size, 128), BF16),
             pltpu.VMEM((macros, 2, size, 128), BF16),
             pltpu.VMEM((ITERS, K, size, 128), F32),

time: 101 us -> 97.3 us (0.963)
  Pallas kernels: 95.5 us -> 92.1 us
    pallas_call x1, Pallas kernels: 95.5 us -> 92.1 us  [on_device(): pl.pallas_call(functools.partial(kernel, dims), out_shape=(jax.ShapeDtype...]
where the time goes in v4:
time: 97.3 us; the launch traced here: 97.2 us
  Pallas kernels  92.1 us (95%)
  local copies, waits for them, and re-layouts  3.76 us (4%)
  between operations  1.3 us (1%)
    pallas_call x1, Pallas kernels, on_device(): pl.pallas_call(functools.partial(kernel, dims), out_shape=(jax.ShapeDtype...  92.1 us
    unnamed x4, local copies, waits for them, and re-layouts  3.76 us

profile of v4, /device:TPU:1, one launch (start us, length us, event | category | flops | bytes accessed | tf_op | source)
XLA Modules:
  0.0 97.2 jit_solution(2637131016580305989)
XLA Ops:
  1.3 92.1 %shard_map.104 = (f32[20,128,128]{2,1,0:T(8,128)}, f32[24,128,128]{2,1,0:T(8,128)}) custom-call(f32[20,128,128]{2,1,0:T(8,128)} %bitcast.39, f32[24,128,128]{2,1,0:T(8,128)} %bitcast.37, bf16[64,256,256]{2,1,0:T(8,128)(2,1)} %bitcast.36, s32[128,128]{1,0:T(8,128)} %bitcast.41, s32[128,128]{1,0:T(8,128)} %bitcast.42, f32[128,128]{1,0:T(8,128)} %bitcast.43, ...), custom_call_target="tpu_custom_call" | custom-call | tf_op jit(solution)/shard_map/pallas_call | solution.py:453
  93.4 0.0 copy-start
  93.4 2.6 %copy.21 = f32[1,20,4,4096]{3,2,1,0:T(4,128)} copy(f32[1,20,4,4096]{3,2,1,0:T(4,128)} %bitcast.40) | data formatting | bytes 2621440
  96.0 0.0 copy-done
  96.0 1.1 %copy.22 = f32[1,24,4,4096]{3,2,1,0:T(4,128)} copy(f32[1,24,4,4096]{3,2,1,0:T(4,128)S(1)} %bitcast.38) | data formatting | bytes 3145728
Async XLA Ops:
  93.4 2.6 %copy-start = (f32[24,128,128]{2,1,0:T(8,128)S(1)}, f32[24,128,128]{2,1,0:T(8,128)}, u32[]{:S(2)}) copy-start(f32[24,128,128]{2,1,0:T(8,128)} %get-tuple-element.5) | copy-start | bytes 4718596

commit v5 on v4

--- a/solution.py
+++ b/solution.py
@@ -61,7 +61,8 @@
 
     barrier = pltpu.get_barrier_semaphore()
 
-    def greet(o, _):
+    def greet(k, _):
+        o = lax.rem(tile + tiles // 2 + k, tiles)
         pl.semaphore_signal(barrier, inc=1, device_id=(1 - member, o), device_id_type=MESH)
         return 0
 
@@ -291,7 +292,7 @@
         lax.fori_loop(0, tiles // 2, pack, 0, unroll=4)
 
         def send(k, _):
-            trace_copy(g, lax.rem(tile + k, tiles)).start()
+            trace_copy(g, lax.rem(tile + tiles // 2 + k, tiles)).start()
             return 0
 
         lax.fori_loop(0, tiles, send, 0, unroll=4)

time: 97.3 us -> 97.4 us (level)
  no operation moved by 1% of the time
where the time goes in v5:
time: 97.4 us; the launch traced here: 97.2 us
  Pallas kernels  92.1 us (95%)
  local copies, waits for them, and re-layouts  3.76 us (4%)
  between operations  1.3 us (1%)
    pallas_call x1, Pallas kernels, on_device(): pl.pallas_call(functools.partial(kernel, dims), out_shape=(jax.ShapeDtype...  92.1 us
    unnamed x4, local copies, waits for them, and re-layouts  3.76 us

profile of v5, /device:TPU:1, one launch (start us, length us, event | category | flops | bytes accessed | tf_op | source)
XLA Modules:
  0.0 97.2 jit_solution(17214188435931507251)
XLA Ops:
  1.3 92.1 %shard_map.104 = (f32[20,128,128]{2,1,0:T(8,128)}, f32[24,128,128]{2,1,0:T(8,128)}) custom-call(f32[20,128,128]{2,1,0:T(8,128)} %bitcast.39, f32[24,128,128]{2,1,0:T(8,128)} %bitcast.37, bf16[64,256,256]{2,1,0:T(8,128)(2,1)} %bitcast.36, s32[128,128]{1,0:T(8,128)} %bitcast.41, s32[128,128]{1,0:T(8,128)} %bitcast.42, f32[128,128]{1,0:T(8,128)} %bitcast.43, ...), custom_call_target="tpu_custom_call" | custom-call | tf_op jit(solution)/shard_map/pallas_call | solution.py:454
  93.4 0.0 copy-start
  93.4 2.6 %copy.21 = f32[1,20,4,4096]{3,2,1,0:T(4,128)} copy(f32[1,20,4,4096]{3,2,1,0:T(4,128)} %bitcast.40) | data formatting | bytes 2621440
  96.0 0.0 copy-done
  96.0 1.1 %copy.22 = f32[1,24,4,4096]{3,2,1,0:T(4,128)} copy(f32[1,24,4,4096]{3,2,1,0:T(4,128)S(1)} %bitcast.38) | data formatting | bytes 3145728
Async XLA Ops:
  93.4 2.6 %copy-start = (f32[24,128,128]{2,1,0:T(8,128)S(1)}, f32[24,128,128]{2,1,0:T(8,128)}, u32[]{:S(2)}) copy-start(f32[24,128,128]{2,1,0:T(8,128)} %get-tuple-element.5) | copy-start | bytes 4718596
